TPU v7x, 128 devices: a whole 4x4x4 slice. The times are simulated.
128 devices in a mesh: north: 32 (over z, x, core), deep: 4 (over y).
Axes of the slice: x: 4, y: 4, z: 4, core: 2. Of those that a mesh axis runs over, the one named last changes fastest.
Arguments:
- source: float32 [512, 512, 2048], P(None, 'north', 'deep'), may hold values from -6 to 6
- symbol_x: float32 [512], replicated, may hold values from 0.3 to 3
- symbol_y: float32 [512], replicated, may hold values from 0.3 to 3
- symbol_z: float32 [2048], replicated, may hold values from 0.3 to 3
Outputs:
- coefficients: float32 [256, 256, 1024], P('north', 'deep')
All inputs are finite; a program needn't handle non-finite values.
Results may differ from a plain program's by a relative error of at most 0.000071.
Values sent between devices are 32-bit elements; how exact they have to be, the bound alone decides.
No kernel may reach another device: no remote copies, remote signals or barrier semaphores. Data moves between devices by JAX's collectives and lax.ppermute only.
A program may use at most 128 MiB of HBM per device.

v0:
```python
import jax
import jax.numpy as jnp
import numpy as np
from jax import lax
from jax.experimental import pallas as pl
from jax.experimental.pallas import tpu as pltpu
from jax.sharding import PartitionSpec as P

F32, BF16 = jnp.float32, jnp.bfloat16
NORTH, DEEP = 32, 4


def sines(rows, modes, count):
    turn = np.outer(np.asarray(rows) + 1, np.asarray(modes) + 1) % (2 * count + 2)
    return np.sin(np.pi / (count + 1) * turn) * (2.0 / (count + 1)) ** 0.5


def halves(table):
    table = np.asarray(table, np.float32)
    high = table.astype(BF16)
    return high, (table - high.astype(np.float32)).astype(BF16)


def wide(table):
    high, low = halves(table)
    return np.concatenate([high, low, high], axis=-1)


def split(values):
    high = values.astype(BF16)
    return high, (values - high.astype(F32)).astype(BF16)


def tall(values):
    high, low = split(values)
    return jnp.concatenate([high, high, low], axis=0)


def dot(a, b):
    return jnp.dot(a, b, preferred_element_type=F32)


def cost(flops, size):
    return pl.CostEstimate(flops=flops, bytes_accessed=size, transcendentals=0)


LIMIT = pltpu.CompilerParams(vmem_limit_bytes=24 * 1024 * 1024)


def vmem():
    return pl.BlockSpec(memory_space=pltpu.VMEM)


def x_kernel(even_ref, odd_ref, x_ref, a_ref, *refs):
    b_refs, (sums, diffs, held, sems) = refs[:DEEP], refs[DEEP:]
    half = x_ref.shape[0] // 2
    me = lax.axis_index("deep")
    step, steps = pl.program_id(0), held.shape[0]
    across = x_ref.shape[2] // 128

    def load(i):
        y, z = pl.multiple_of(i // across * 8, 8), pl.multiple_of(i % across * 128, 128)
        return pltpu.make_async_copy(x_ref.at[:, pl.ds(y, 8), pl.ds(z, 128)], held.at[i], sems.at[i])

    @pl.when(step == 0)
    def _():
        for i in range(steps):
            load(i).start()

    load(step).wait()

    def fold(t, carry):
        for j in range(32):
            i = t * 32 + j
            near, far = held[step, i], held[step, 2 * half - 1 - i]
            sums[pl.ds(pl.multiple_of(i * 8, 8), 8), :] = near + far
            diffs[pl.ds(pl.multiple_of(i * 8, 8), 8), :] = near - far
        return carry

    lax.fori_loop(0, half // 32, fold, 0)
    even = even_ref[...]
    odd = jnp.concatenate([odd_ref[me ^ k] for k in range(DEEP)], axis=0)
    a_rows = a_ref.reshape(half // 2 * 8, 128)
    b_rows = [b.reshape(NORTH * 8, 128) for b in b_refs]
    for y in range(0, 8, 2):
        s = jnp.concatenate([sums[pl.ds(y + j, half, stride=8), :] for j in range(2)], axis=1)
        e = dot(even, tall(s))
        t = jnp.concatenate([diffs[pl.ds(y + j, half, stride=8), :] for j in range(2)], axis=1)
        o = dot(odd, tall(t))
        for j in range(2):
            a_rows[pl.ds(y + j, half // 2, stride=8), :] = e[:, j * 128 : (j + 1) * 128]
            for k in range(DEEP):
                b_rows[k][pl.ds(y + j, NORTH, stride=8), :] = o[k * NORTH : (k + 1) * NORTH, j * 128 : (j + 1) * 128]


def x_stage(source):
    nx, ny, nz = source.shape
    modes = nx // 2
    block = modes // NORTH
    near = np.arange(nx // 2)
    even = wide(sines(near, np.arange(0, modes, 2), nx).T)
    odd_modes = (block * np.arange(NORTH)[None, :] + 2 * np.arange(DEEP)[:, None] + 1).reshape(-1)
    odd = wide(sines(near, odd_modes, nx).T).reshape(DEEP, NORTH, -1)
    across = nz // 128
    steps = ny // 8 * across
    b_shape = jax.ShapeDtypeStruct((NORTH, ny, nz), F32)
    b_spec = pl.BlockSpec((NORTH, 8, 128), lambda i: (0, i // across, i % across))
    return pl.pallas_call(
        x_kernel,
        grid=(steps,),
        in_specs=[vmem(), vmem(), pl.BlockSpec(memory_space=pl.ANY)],
        out_specs=[pl.BlockSpec((modes // 2, 8, 128), lambda i: (0, i // across, i % across))] + [b_spec] * DEEP,
        out_shape=[jax.ShapeDtypeStruct((modes // 2, ny, nz), F32)] + [b_shape] * DEEP,
        scratch_shapes=[pltpu.VMEM((nx // 2 * 8, 128), F32)] * 2
        + [pltpu.VMEM((steps, nx, 8, 128), F32), pltpu.SemaphoreType.DMA((steps,))],
        cost_estimate=cost(6 * nx * modes * ny * nz // 2, 6 * nx * ny * nz),
        name="x_stage",
    )(jnp.asarray(even), jnp.asarray(odd), source)


def y_table(ny):
    return jnp.asarray(wide(sines(np.arange(ny), np.arange(ny // 2), ny).T).reshape(DEEP, ny // 2 // DEEP, -1))


def ya_kernel(table_ref, v_ref, *outs):
    me = lax.axis_index("deep")
    table = jnp.concatenate([table_ref[me ^ k] for k in range(DEEP)], axis=0)
    v = v_ref[...]
    n, _, y, z = v.shape
    r = dot(table, tall(v.reshape(n * y, z)))
    m = r.shape[0] // DEEP
    for k in range(DEEP):
        outs[k][0] = r[k * m : (k + 1) * m]


def ya_stage(table, v):
    n, js, y, nz = v.shape
    m = table.shape[1]
    zb = 256
    return pl.pallas_call(
        ya_kernel,
        grid=(js, nz // zb),
        in_specs=[vmem(), pl.BlockSpec((n, 1, y, zb), lambda j, z: (0, j, 0, z))],
        out_specs=[pl.BlockSpec((1, m, zb), lambda j, z: (j, 0, z))] * DEEP,
        out_shape=[jax.ShapeDtypeStruct((js, m, nz), F32)] * DEEP,
        cost_estimate=cost(6 * n * y * m * DEEP * js * nz, 6 * n * js * y * nz),
        compiler_params=LIMIT,
        name="ya_stage",
    )(table, v)


def backwards(v):
    lanes = v.shape[-1] // 128
    at = 127 - lax.broadcasted_iota(jnp.int32, (v.shape[0], 128), 1)
    parts = [v[:, i * 128 : (i + 1) * 128] for i in range(lanes)]
    return jnp.concatenate([jnp.take_along_axis(p, at, axis=1) for p in parts[::-1]], axis=1)


def shuffled(even, odd):
    lane = lax.broadcasted_iota(jnp.int32, (even.shape[0], 128), 1)
    parts = []
    for i in range(even.shape[1] // 128):
        e, o = even[:, i * 128 : (i + 1) * 128], odd[:, i * 128 : (i + 1) * 128]
        for at in (lane // 2, lane // 2 + 64):
            e_at, o_at = jnp.take_along_axis(e, at, axis=1), jnp.take_along_axis(o, at, axis=1)
            parts.append(jnp.where(lane % 2 == 0, e_at, o_at))
    return jnp.concatenate(parts, axis=1)


def z_halves(near, far, table):
    far = backwards(far)
    count = near.shape[0]
    both = []
    for parity, v in enumerate((near + far, near - far)):
        high, low = split(v)
        r = dot(jnp.concatenate([high, low], axis=0), table[parity, 0])
        both.append(r[:count] + r[count:] + dot(high, table[parity, 1]))
    return both


def zb_kernel(table_ref, near_ref, far_ref, *rest):
    n, y, z = near_ref.shape
    even, odd = z_halves(near_ref[...].reshape(n * y, z), far_ref[...].reshape(n * y, z), table_ref)
    *before, o_ref = rest
    half = even.shape[1]
    even, odd = even.reshape(n, y, half), odd.reshape(n, y, half)
    if before:
        even, odd = even + before[0][:, :, :half], odd + before[0][:, :, half:]
    o_ref[:, :, :half] = even
    o_ref[:, :, half:] = odd


def zb_stage(table, near, far, *before):
    n, y, z = near.shape
    modes, rows = 2 * table.shape[3], 8
    spec = pl.BlockSpec((rows, y, z), lambda i: (i, 0, 0))
    wide_spec = pl.BlockSpec((rows, y, modes), lambda i: (i, 0, 0))
    return pl.pallas_call(
        zb_kernel,
        grid=(n // rows,),
        in_specs=[vmem(), spec, spec] + [wide_spec] * len(before),
        out_specs=wide_spec,
        out_shape=pltpu.HBM((n, y, modes), F32) if before else jax.ShapeDtypeStruct((n, y, modes), F32),
        cost_estimate=cost(6 * n * y * z * modes, 8 * n * y * (z + modes)),
        compiler_params=LIMIT,
        name="zb_stage",
    )(table, near, far, *before)


def za_kernel(sx_ref, t0_ref, t1_ref, sy_ref, sz_ref, p0, p1, p2, p3, o_ref):
    m, z = p0.shape[1], p0.shape[2]
    even0, odd0 = z_halves(p0[...].reshape(m, z), p3[...].reshape(m, z), t0_ref)
    even1, odd1 = z_halves(p1[...].reshape(m, z), p2[...].reshape(m, z), t1_ref)
    total = shuffled(even0 + even1, odd0 + odd1)
    yz = jnp.concatenate([sy_ref[lax.axis_index("deep")]] * (o_ref.shape[3] // 128), axis=1) + sz_ref[...]
    first = lax.axis_index("north") * 2 * pl.num_programs(0)
    o_ref[0, 0] = total * lax.rsqrt(sx_ref[first + 2 * pl.program_id(0)] + yz)


def za_stage(sx, tables, sy, sz, pieces):
    js, m, z = pieces[0].shape
    modes = 2 * tables[0].shape[3]
    spec = pl.BlockSpec((1, m, z), lambda j: (j, 0, 0))
    return pl.pallas_call(
        za_kernel,
        grid=(js,),
        in_specs=[pl.BlockSpec(memory_space=pltpu.SMEM)] + [vmem()] * 4 + [spec] * DEEP,
        out_specs=pl.BlockSpec((1, 1, m, modes), lambda j: (j, 0, 0, 0)),
        out_shape=jax.ShapeDtypeStruct((js, 2, m, modes), F32),
        cost_estimate=cost(6 * js * m * z * 2 * modes, 4 * js * m * z * DEEP + 8 * z * modes),
        compiler_params=LIMIT,
        name="za_stage",
    )(sx, *tables, sy, sz, *pieces)


def yb_kernel(sx_ref, table_ref, sy_ref, sz_ref, even_ref, odd_ref, *outs):
    me = lax.axis_index("deep")
    table = jnp.concatenate([table_ref[me ^ k] for k in range(DEEP)], axis=0)
    n, y, z = even_ref.shape
    e = dot(table, tall(even_ref[...].reshape(n * y, z)))
    o = dot(table, tall(odd_ref[...].reshape(n * y, z)))
    m = table.shape[0] // DEEP
    sx = sx_ref[lax.axis_index("north") * 2 * DEEP + 2 * me + 1]
    for k in range(DEEP):
        symbol = sx + jnp.concatenate([sy_ref[me ^ k]] * (2 * z // 128), axis=1) + sz_ref[...]
        outs[k][...] = shuffled(e[k * m : (k + 1) * m], o[k * m : (k + 1) * m]) * lax.rsqrt(symbol)


def yb_stage(sx, table, sy, sz, v):
    n, y, modes = v.shape
    m, block = table.shape[1], 512
    steps = modes // block
    return pl.pallas_call(
        yb_kernel,
        grid=(steps,),
        in_specs=[
            pl.BlockSpec(memory_space=pltpu.SMEM),
            vmem(),
            vmem(),
            pl.BlockSpec((1, block), lambda i: (0, i)),
            pl.BlockSpec((n, y, block // 2), lambda i: (0, 0, i)),
            pl.BlockSpec((n, y, block // 2), lambda i: (0, 0, i + 2)),
        ],
        out_specs=[pl.BlockSpec((m, block), lambda i: (0, i))] * DEEP,
        out_shape=[jax.ShapeDtypeStruct((m, modes), F32)] * DEEP,
        cost_estimate=cost(6 * n * y * m * DEEP * modes, 6 * n * y * modes),
        compiler_params=LIMIT,
        name="yb_stage",
    )(sx, table, sy, sz, v, v)


def join_kernel(whole_ref, p0, p1, p2, p3, o_ref, sems):
    me = lax.axis_index("deep")
    copies = [
        pltpu.make_async_copy(p, o_ref.at[me ^ k, 1], sems.at[k]) for k, p in enumerate((p0, p1, p2, p3))
    ]
    for copy in copies:
        copy.start()
    for copy in copies:
        copy.wait()


def join_stage(whole, pieces):
    return pl.pallas_call(
        join_kernel,
        in_specs=[pl.BlockSpec(memory_space=pl.ANY)] + [vmem()] * DEEP,
        out_specs=pl.BlockSpec(memory_space=pl.ANY),
        out_shape=jax.ShapeDtypeStruct(whole.shape, F32),
        scratch_shapes=[pltpu.SemaphoreType.DMA((DEEP,))],
        input_output_aliases={0: 0},
        cost_estimate=cost(1, 8 * pieces[0].size * DEEP),
        compiler_params=LIMIT,
        name="join_stage",
    )(whole, *pieces)


def z_table(count, pair):
    stretch = lax.axis_index("deep") ^ pair
    point = (stretch * (count // DEEP) + jnp.arange(count // DEEP))[None, :, None]
    mode = (2 * jnp.arange(count // 4) + jnp.arange(2)[:, None])[:, None, :]
    turn = (point + 1) * (mode + 1) % (2 * count + 2)
    table = jnp.sin(np.float32(np.pi / (count + 1)) * turn.astype(F32)) * np.float32((2.0 / (count + 1)) ** 0.5)
    high = lax.reduce_precision(table, 8, 7)
    return jnp.stack([high, table - high], axis=1).astype(BF16)


def deep_exchange(pieces):
    got = [pieces[0]] + [None] * (DEEP - 1)
    for k in (1, 3, 2):
        got[k] = lax.ppermute(pieces[k], "deep", [(s, s ^ k) for s in range(DEEP)])
    return got


def north_exchange(v):
    return lax.all_to_all(v, "north", split_axis=0, concat_axis=0, tiled=True)


def on_device(source, symbol_x, symbol_y, symbol_z):
    ny, nz = source.shape[1] * NORTH, source.shape[2] * DEEP
    a, *b = x_stage(source)
    b = deep_exchange(b)
    a = north_exchange(a.reshape(NORTH, -1, *a.shape[1:]))
    tz = [z_table(nz, q) for q in range(2)]
    ty = y_table(ny)
    sy = jnp.broadcast_to(symbol_y[: ny // 2, None], (ny // 2, 128)).reshape(DEEP, -1, 128)
    sz = symbol_z[None, : nz // 2]
    part = zb_stage(tz[0], b[0], b[3])
    part = zb_stage(tz[1], b[1], b[2], part)
    b = north_exchange(part)
    a = deep_exchange(ya_stage(ty, a))
    whole = za_stage(symbol_x, tz, sy, sz, a)
    b = deep_exchange(yb_stage(symbol_x, ty, sy, sz, b))
    whole = join_stage(whole, b)
    return whole.reshape(-1, *whole.shape[2:])


def solution(mesh):
    in_specs = (P(None, "north", "deep"), P(), P(), P())
    out_specs = P("north", "deep", None)
    return jax.shard_map(on_device, mesh=mesh, in_specs=in_specs, out_specs=out_specs, check_vma=False)
```

profile of v0, /device:TPU:1, one launch (start us, length us, event | category | flops | bytes accessed | tf_op | source)
XLA Modules:
  0.0 137.2 jit_solution(15015377792414378009)
XLA Ops:
  0.0 13.8 %x_stage.1 = (f32[128,16,512]{2,1,0:T(8,128)}, f32[32,16,512]{2,1,0:T(8,128)}, f32[32,16,512]{2,1,0:T(8,128)}, f32[32,16,512]{2,1,0:T(8,128)}, f32[32,16,512]{2,1,0:T(8,128)}) custom-call(bf16[128,768]{1,0:T(8,128)(2,1)} %constant.37.clone.even_ref, bf16[4,32,768]{2,1,0:T(8,128)(2,1)} %constant.38.clone.odd_ref, f32[512,16,512]{2,1,0:T(8,128)} %x_ref.1), custom_call_target="tpu_custom_call" | custom-call | flops 3221225472 | bytes 25165824 | tf_op jit(solution)/shard_map/x_stage/pallas_call | solution.py:108
  13.8 9.5 %all-to-all-start = ((f32[32,4,16,512]{3,2,1,0:T(8,128)}), f32[32,4,16,512]{3,2,1,0:T(8,128)}, u32[]{:S(2)}, u32[]{:S(2)}) async-start(f32[32,4,16,512]{3,2,1,0:T(8,128)} %bitcast.5), calls=%async_computation | async-start | bytes 8388608 | tf_op jit(solution)/shard_map/all_to_all | solution.py:315
  23.3 2.8 %collective-permute-start.5 = (f32[32,16,512]{2,1,0:T(8,128)}, f32[32,16,512]{2,1,0:T(8,128)S(1)}, u32[]{:S(2)}, u32[]{:S(2)}) collective-permute-start(f32[32,16,512]{2,1,0:T(8,128)} %get-tuple-element.26), channel_id=1, source_target_pairs={{0,3},{1,2},{2,1},{3,0},{4,7},{5,6},{6,5},{7,4},{8,11},{9,10},{10,... | collective-permute-start | bytes 3145736 | tf_op jit(solution)/shard_map/ppermute | solution.py:310
  26.1 0.0 collective-permute-start.3
  26.1 1.3 collective-permute-start.4
  27.4 17.2 %reduce-precision_convert_fusion = (bf16[2,1,512,512]{3,2,1,0:T(8,128)(2,1)S(1)}, bf16[2,1,512,512]{3,2,1,0:T(8,128)(2,1)S(1)}, bf16[2,1,512,512]{3,2,1,0:T(8,128)(2,1)S(1)}, bf16[2,1,512,512]{3,2,1,0:T(8,128)(2,1)S(1)}) fusion(s32[512]{0:T(512)S(1)} %get-tuple-element.37, s32[2,512]{1,0:T(2,128)S(1)} %add_add_fusion, s32[512]{0:T(512)S(1)} %get-tuple-element.38), kind=kLoop, calls=%fused_computation.3 | loop fusion | flops 14680064 | bytes 4202496 | tf_op jit(solution)/shard_map/convert
  44.7 0.2 pad_maximum_fusion.1.t1_ref.table_ref
  44.9 0.0 copy-start
  44.9 0.0 copy-start.2
  44.9 0.2 pad_maximum_fusion.t0_ref.table_ref
  45.1 4.4 %collective-permute-done.5.far_ref = f32[32,16,512]{2,1,0:T(8,128)S(1)} collective-permute-done((f32[32,16,512]{2,1,0:T(8,128)}, f32[32,16,512]{2,1,0:T(8,128)S(1)}, u32[]{:S(2)}, u32[]{:S(2)}) %collective-permute-start.5) | collective-permute-done | bytes 1048608 | tf_op jit(solution)/shard_map/ppermute | solution.py:310
  49.5 0.0 copy-done.2
  49.5 2.5 %zb_stage.2.rest_0_ = f32[32,16,1024]{2,1,0:T(8,128)S(1)} custom-call(bf16[2,2,512,512]{3,2,1,0:T(8,128)(2,1)S(1)} %pad_maximum_fusion.t0_ref.table_ref, f32[32,16,512]{2,1,0:T(8,128)S(1)} %copy-done.2, f32[32,16,512]{2,1,0:T(8,128)S(1)} %collective-permute-done.5.far_ref), custom_call_target="tpu_custom_call" | custom-call | flops 1610612736 | bytes 6291456 | tf_op jit(solution)/shard_map/zb_stage/pallas_call | solution.py:198
  52.0 0.0 collective-permute-done.3.near_ref
  52.0 21.0 %collective-permute-done.4.far_ref = f32[32,16,512]{2,1,0:T(8,128)} collective-permute-done((f32[32,16,512]{2,1,0:T(8,128)}, f32[32,16,512]{2,1,0:T(8,128)}, u32[]{:S(2)}, u32[]{:S(2)}) %collective-permute-start.4) | collective-permute-done | bytes 1048608 | tf_op jit(solution)/shard_map/ppermute | solution.py:310
  73.0 0.0 copy-done
  73.0 5.0 %zb_stage.3 = f32[32,16,1024]{2,1,0:T(8,128)} custom-call(bf16[2,2,512,512]{3,2,1,0:T(8,128)(2,1)S(1)} %pad_maximum_fusion.1.t1_ref.table_ref, f32[32,16,512]{2,1,0:T(8,128)} %collective-permute-done.3.near_ref, f32[32,16,512]{2,1,0:T(8,128)} %collective-permute-done.4.far_ref, f32[32,16,1024]{2,1,0:T(8,128)S(1)} %zb_stage.2.rest_0_), custom_call_target="tpu_custom_call" | custom-call | flops 1610612736 | bytes 6291456 | tf_op jit(solution)/shard_map/zb_stage/pallas_call | solution.py:198
  78.0 0.0 copy-start.3
  78.0 0.0 all-to-all-done.v_ref
  78.0 8.5 %all-to-all-start.1 = ((f32[32,16,1024]{2,1,0:T(8,128)}), f32[32,16,1024]{2,1,0:T(8,128)}, u32[]{:S(2)}, u32[]{:S(2)}) async-start(f32[32,16,1024]{2,1,0:T(8,128)} %zb_stage.3), calls=%async_computation.1 | async-start | bytes 4194304 | tf_op jit(solution)/shard_map/all_to_all | solution.py:315
  86.5 0.0 copy-done.3
  86.5 0.0 slice-start
  86.5 0.0 copy-start.5
  86.6 0.0 copy-start.4
  86.6 7.5 %ya_stage.1 = (f32[4,64,512]{2,1,0:T(8,128)S(1)}, f32[4,64,512]{2,1,0:T(8,128)}, f32[4,64,512]{2,1,0:T(8,128)}, f32[4,64,512]{2,1,0:T(8,128)}) custom-call(bf16[4,64,1536]{2,1,0:T(8,128)(2,1)S(1)} %copy-done.3, f32[32,4,16,512]{3,2,1,0:T(8,128)} %all-to-all-done.v_ref), custom_call_target="tpu_custom_call" | custom-call | flops 1610612736 | bytes 6291456 | tf_op jit(solution)/shard_map/ya_stage/pallas_call | solution.py:140
  94.0 0.0 collective-permute-start
  94.0 3.8 %collective-permute-start.1 = (f32[4,64,512]{2,1,0:T(8,128)}, f32[4,64,512]{2,1,0:T(8,128)}, u32[]{:S(2)}, u32[]{:S(2)}) collective-permute-start(f32[4,64,512]{2,1,0:T(8,128)} %get-tuple-element.21), channel_id=1, source_target_pairs={{0,2},{1,3},{2,0},{3,1},{4,6},{5,7},{6,4},{7,5},{8,10},{9,11},{10,... | collective-permute-start | bytes 1572872 | tf_op jit(solution)/shard_map/ppermute | solution.py:310
  97.8 0.1 collective-permute-start.2
  97.9 0.0 slice-done
  97.9 0.1 broadcast_in_dim.6
  98.0 0.0 copy-done.5
  98.0 17.3 %all-to-all-done.1.even_ref.odd_ref = f32[32,16,1024]{2,1,0:T(8,128)} async-done(((f32[32,16,1024]{2,1,0:T(8,128)}), f32[32,16,1024]{2,1,0:T(8,128)}, u32[]{:S(2)}, u32[]{:S(2)}) %all-to-all-start.1) | async-done | bytes 2097184 | tf_op jit(solution)/shard_map/all_to_all | solution.py:315
  115.2 0.1 broadcast_in_dim.7.sy_ref
  115.3 0.0 copy-done.4
  115.4 0.0 copy-start.1
  115.4 3.6 %yb_stage.1 = (f32[64,1024]{1,0:T(8,128)S(1)}, f32[64,1024]{1,0:T(8,128)S(1)}, f32[64,1024]{1,0:T(8,128)S(1)}, f32[64,1024]{1,0:T(8,128)S(1)}) custom-call(f32[512]{0:T(512)S(1)} %copy-done.4, bf16[4,64,1536]{2,1,0:T(8,128)(2,1)S(1)} %copy-done.3, f32[4,64,128]{2,1,0:T(8,128)S(1)} %broadcast_in_dim.7.sy_ref, f32[1,1024]{1,0:T(1,128)S(1)} %bitcast.3, ...), custom_call_target="tpu_custom_call" | custom-call | flops 805306368 | bytes 3145728 | tf_op jit(solution)/shard_map/yb_stage/pallas_call | solution.py:253
  119.0 0.1 collective-permute-start.6
  119.0 3.8 %collective-permute-start.7 = (f32[64,1024]{1,0:T(8,128)S(1)}, f32[64,1024]{1,0:T(8,128)S(1)}, u32[]{:S(2)}, u32[]{:S(2)}) collective-permute-start(f32[64,1024]{1,0:T(8,128)S(1)} %get-tuple-element.29), channel_id=1, source_target_pairs={{0,2},{1,3},{2,0},{3,1},{4,6},{5,7},{6,4},{7,5},{8,10},{9,11},{10,... | collective-permute-start | bytes 786440 | tf_op jit(solution)/shard_map/ppermute | solution.py:310
  122.8 0.0 collective-permute-done.p1
  122.8 0.1 collective-permute-start.8
  122.9 0.0 collective-permute-done.1.p2
  122.9 0.3 collective-permute-done.2.p3
  123.2 0.0 copy-done.1
  123.2 5.9 %za_stage.1.whole_ref = f32[4,2,64,1024]{3,2,1,0:T(8,128)} custom-call(f32[512]{0:T(512)S(1)} %copy-done.4, bf16[2,2,512,512]{3,2,1,0:T(8,128)(2,1)S(1)} %pad_maximum_fusion.t0_ref.table_ref, bf16[2,2,512,512]{3,2,1,0:T(8,128)(2,1)S(1)} %copy-done.1, f32[4,64,128]{2,1,0:T(8,128)S(1)} %broadcast_in_dim.7.sy_ref, f32[1,1024]{1,0:T(1,128)S(1)} %bitcast.4, ...), custom_call_target="tpu_custom_call" | custom-call | flops 1610612736 | bytes 6291456 | tf_op jit(solution)/shard_map/za_stage/pallas_call | solution.py:224
  129.1 0.0 collective-permute-done.6.p1
  129.1 4.1 %collective-permute-done.7.p2 = f32[64,1024]{1,0:T(8,128)S(1)} collective-permute-done((f32[64,1024]{1,0:T(8,128)S(1)}, f32[64,1024]{1,0:T(8,128)S(1)}, u32[]{:S(2)}, u32[]{:S(2)}) %collective-permute-start.7) | collective-permute-done | bytes 262176 | tf_op jit(solution)/shard_map/ppermute | solution.py:310
  133.2 3.0 %collective-permute-done.8.p3 = f32[64,1024]{1,0:T(8,128)S(1)} collective-permute-done((f32[64,1024]{1,0:T(8,128)S(1)}, f32[64,1024]{1,0:T(8,128)S(1)}, u32[]{:S(2)}, u32[]{:S(2)}) %collective-permute-start.8) | collective-permute-done | bytes 262176 | tf_op jit(solution)/shard_map/ppermute | solution.py:310
  136.2 1.0 join_stage.1
  (4 shorter events, 0.0 us)
Async XLA Ops:
  13.8 64.2 %all-to-all-start = ((f32[32,4,16,512]{3,2,1,0:T(8,128)}), f32[32,4,16,512]{3,2,1,0:T(8,128)}, u32[]{:S(2)}, u32[]{:S(2)}) async-start(f32[32,4,16,512]{3,2,1,0:T(8,128)} %bitcast.5), calls=%async_computation | async-start | bytes 8388608 | tf_op jit(solution)/shard_map/all_to_all | solution.py:315
  23.3 26.1 %collective-permute-start.5 = (f32[32,16,512]{2,1,0:T(8,128)}, f32[32,16,512]{2,1,0:T(8,128)S(1)}, u32[]{:S(2)}, u32[]{:S(2)}) collective-permute-start(f32[32,16,512]{2,1,0:T(8,128)} %get-tuple-element.26), channel_id=1, source_target_pairs={{0,3},{1,2},{2,1},{3,0},{4,7},{5,6},{6,5},{7,4},{8,11},{9,10},{10,... | collective-permute-start | bytes 3145736 | tf_op jit(solution)/shard_map/ppermute | solution.py:310
  26.1 25.8 %collective-permute-start.3 = (f32[32,16,512]{2,1,0:T(8,128)}, f32[32,16,512]{2,1,0:T(8,128)}, u32[]{:S(2)}, u32[]{:S(2)}) collective-permute-start(f32[32,16,512]{2,1,0:T(8,128)} %get-tuple-element.23), channel_id=1, source_target_pairs={{0,1},{1,0},{2,3},{3,2},{4,5},{5,4},{6,7},{7,6},{8,9},{9,8},{10,11... | collective-permute-start | bytes 3145736 | tf_op jit(solution)/shard_map/ppermute | solution.py:310
  26.1 46.9 %collective-permute-start.4 = (f32[32,16,512]{2,1,0:T(8,128)}, f32[32,16,512]{2,1,0:T(8,128)}, u32[]{:S(2)}, u32[]{:S(2)}) collective-permute-start(f32[32,16,512]{2,1,0:T(8,128)} %get-tuple-element.24), channel_id=1, source_target_pairs={{0,2},{1,3},{2,0},{3,1},{4,6},{5,7},{6,4},{7,5},{8,10},{9,11},{10,... | collective-permute-start | bytes 3145736 | tf_op jit(solution)/shard_map/ppermute | solution.py:310
  44.9 28.1 %copy-start = (bf16[2,2,512,512]{3,2,1,0:T(8,128)(2,1)}, bf16[2,2,512,512]{3,2,1,0:T(8,128)(2,1)S(1)}, u32[]{:S(2)}) copy-start(bf16[2,2,512,512]{3,2,1,0:T(8,128)(2,1)S(1)} %pad_maximum_fusion.1.t1_ref.table_ref) | copy-start | bytes 6291460
  44.9 4.6 %copy-start.2 = (f32[32,16,512]{2,1,0:T(8,128)S(1)}, f32[32,16,512]{2,1,0:T(8,128)}, u32[]{:S(2)}) copy-start(f32[32,16,512]{2,1,0:T(8,128)} %get-tuple-element.25.near_ref) | copy-start | bytes 3145732
  78.0 8.5 %copy-start.3 = (bf16[4,64,1536]{2,1,0:T(8,128)(2,1)S(1)}, bf16[4,64,1536]{2,1,0:T(8,128)(2,1)}, u32[]{:S(2)}) copy-start(bf16[4,64,1536]{2,1,0:T(8,128)(2,1)} %constant.39.clone.table_ref) | copy-start | bytes 2359300
  78.0 37.2 %all-to-all-start.1 = ((f32[32,16,1024]{2,1,0:T(8,128)}), f32[32,16,1024]{2,1,0:T(8,128)}, u32[]{:S(2)}, u32[]{:S(2)}) async-start(f32[32,16,1024]{2,1,0:T(8,128)} %zb_stage.3), calls=%async_computation.1 | async-start | bytes 4194304 | tf_op jit(solution)/shard_map/all_to_all | solution.py:315
  86.5 11.4 %slice-start = ((f32[512]{0:T(512)}), f32[256]{0:T(256)S(1)}, s32[]{:S(2)}) async-start(f32[512]{0:T(512)} %param.9), calls=%async_computation.2 | async-start | bytes 2048 | tf_op jit(solution)/shard_map/slice | solution.py:325
  86.5 11.4 %copy-start.5 = (f32[2048]{0:T(1024)S(1)}, f32[2048]{0:T(1024)}, u32[]{:S(2)}) copy-start(f32[2048]{0:T(1024)} %param.10) | copy-start | bytes 24580
  86.6 28.8 %copy-start.4 = (f32[512]{0:T(512)S(1)}, f32[512]{0:T(512)}, u32[]{:S(2)}) copy-start(f32[512]{0:T(512)} %sx_ref.3) | copy-start | bytes 6148
  94.0 28.8 %collective-permute-start = (f32[4,64,512]{2,1,0:T(8,128)}, f32[4,64,512]{2,1,0:T(8,128)}, u32[]{:S(2)}, u32[]{:S(2)}) collective-permute-start(f32[4,64,512]{2,1,0:T(8,128)} %get-tuple-element.20), channel_id=1, source_target_pairs={{0,1},{1,0},{2,3},{3,2},{4,5},{5,4},{6,7},{7,6},{8,9},{9,8},{10,11... | collective-permute-start | bytes 1572872 | tf_op jit(solution)/shard_map/ppermute | solution.py:310
  94.0 28.9 %collective-permute-start.1 = (f32[4,64,512]{2,1,0:T(8,128)}, f32[4,64,512]{2,1,0:T(8,128)}, u32[]{:S(2)}, u32[]{:S(2)}) collective-permute-start(f32[4,64,512]{2,1,0:T(8,128)} %get-tuple-element.21), channel_id=1, source_target_pairs={{0,2},{1,3},{2,0},{3,1},{4,6},{5,7},{6,4},{7,5},{8,10},{9,11},{10,... | collective-permute-start | bytes 1572872 | tf_op jit(solution)/shard_map/ppermute | solution.py:310
  97.8 25.4 %collective-permute-start.2 = (f32[4,64,512]{2,1,0:T(8,128)}, f32[4,64,512]{2,1,0:T(8,128)}, u32[]{:S(2)}, u32[]{:S(2)}) collective-permute-start(f32[4,64,512]{2,1,0:T(8,128)} %get-tuple-element.22), channel_id=1, source_target_pairs={{0,3},{1,2},{2,1},{3,0},{4,7},{5,6},{6,5},{7,4},{8,11},{9,10},{10,... | collective-permute-start | bytes 1572872 | tf_op jit(solution)/shard_map/ppermute | solution.py:310
  115.4 7.8 %copy-start.1 = (bf16[2,2,512,512]{3,2,1,0:T(8,128)(2,1)S(1)}, bf16[2,2,512,512]{3,2,1,0:T(8,128)(2,1)}, u32[]{:S(2)}) copy-start(bf16[2,2,512,512]{3,2,1,0:T(8,128)(2,1)} %copy-done) | copy-start | bytes 6291460
  119.0 10.2 %collective-permute-start.6 = (f32[64,1024]{1,0:T(8,128)S(1)}, f32[64,1024]{1,0:T(8,128)S(1)}, u32[]{:S(2)}, u32[]{:S(2)}) collective-permute-start(f32[64,1024]{1,0:T(8,128)S(1)} %get-tuple-element.28), channel_id=1, source_target_pairs={{0,1},{1,0},{2,3},{3,2},{4,5},{5,4},{6,7},{7,6},{8,9},{9,8},{10,11... | collective-permute-start | bytes 786440 | tf_op jit(solution)/shard_map/ppermute | solution.py:310
  119.0 14.2 %collective-permute-start.7 = (f32[64,1024]{1,0:T(8,128)S(1)}, f32[64,1024]{1,0:T(8,128)S(1)}, u32[]{:S(2)}, u32[]{:S(2)}) collective-permute-start(f32[64,1024]{1,0:T(8,128)S(1)} %get-tuple-element.29), channel_id=1, source_target_pairs={{0,2},{1,3},{2,0},{3,1},{4,6},{5,7},{6,4},{7,5},{8,10},{9,11},{10,... | collective-permute-start | bytes 786440 | tf_op jit(solution)/shard_map/ppermute | solution.py:310
  122.8 13.4 %collective-permute-start.8 = (f32[64,1024]{1,0:T(8,128)S(1)}, f32[64,1024]{1,0:T(8,128)S(1)}, u32[]{:S(2)}, u32[]{:S(2)}) collective-permute-start(f32[64,1024]{1,0:T(8,128)S(1)} %get-tuple-element.30), channel_id=1, source_target_pairs={{0,3},{1,2},{2,1},{3,0},{4,7},{5,6},{6,5},{7,4},{8,11},{9,10},{10,... | collective-permute-start | bytes 786440 | tf_op jit(solution)/shard_map/ppermute | solution.py:310
where the time goes:
time: 139 us; the launch traced here: 137 us
  waiting for transfers between devices  50 us (36%)
  Pallas kernels  39.3 us (28%)
  starting transfers between devices  29.9 us (22%)
  other arithmetic  17.6 us (13%)
    ppermute x9, waiting for transfers between devices, deep_exchange(): got[k] = lax.ppermute(pieces[k], 'deep', [(s, s ^ k) for s in range(DEEP)])  32.7 us
    all_to_all x2, starting transfers between devices, north_exchange(): return lax.all_to_all(v, 'north', split_axis=0, concat_axis=0, tiled=True)  18 us
    all_to_all x2, waiting for transfers between devices, north_exchange(): return lax.all_to_all(v, 'north', split_axis=0, concat_axis=0, tiled=True)  17.3 us
    another operation x1, other arithmetic  17.2 us
    pallas_call x1, Pallas kernels, x_stage(): pl.pallas_call(x_kernel, grid=(steps,), in_specs=[vmem(), vmem(), pl.Bloc...  13.8 us
    ppermute x9, starting transfers between devices, deep_exchange(): got[k] = lax.ppermute(pieces[k], 'deep', [(s, s ^ k) for s in range(DEEP)])  11.9 us
    pallas_call x2, Pallas kernels, zb_stage(): pl.pallas_call(zb_kernel, grid=(n // rows,), in_specs=[vmem(), spec, spec...  7.51 us
    pallas_call x1, Pallas kernels, ya_stage(): pl.pallas_call(ya_kernel, grid=(js, nz // zb), in_specs=[vmem(), pl.Block...  7.45 us
  transfers between devices with their start and end apart: 11, of which 6 were waited for; matrix products, arithmetic and copies ran while one was open for 13% of the time, Pallas kernels for 18%

commit v1 on v0

--- a/solution.py
+++ b/solution.py
@@ -40,6 +40,13 @@
     return jnp.dot(a, b, preferred_element_type=F32)
 
 
+def product(table, values):
+    count = table.shape[0] // 2
+    high, low = split(values)
+    r = dot(table, high)
+    return r[:count] + r[count:] + dot(table[:count], low)
+
+
 def cost(flops, size):
     return pl.CostEstimate(flops=flops, bytes_accessed=size, transcendentals=0)
 
@@ -51,46 +58,56 @@
     return pl.BlockSpec(memory_space=pltpu.VMEM)
 
 
+def upside_down(v):
+    at = 7 - lax.broadcasted_iota(jnp.int32, (8, v.shape[1]), 0)
+    parts = [jnp.take_along_axis(v[i : i + 8], at, axis=0) for i in range(0, v.shape[0], 8)]
+    return jnp.concatenate(parts[::-1], axis=0)
+
+
 def x_kernel(even_ref, odd_ref, x_ref, a_ref, *refs):
-    b_refs, (sums, diffs, held, sems) = refs[:DEEP], refs[DEEP:]
+    b_refs, (held, sems) = refs[:DEEP], refs[DEEP:]
     half = x_ref.shape[0] // 2
     me = lax.axis_index("deep")
-    step, steps = pl.program_id(0), held.shape[0]
+    step, steps, slots = pl.program_id(0), pl.num_programs(0), held.shape[0]
     across = x_ref.shape[2] // 128
 
     def load(i):
         y, z = pl.multiple_of(i // across * 8, 8), pl.multiple_of(i % across * 128, 128)
-        return pltpu.make_async_copy(x_ref.at[:, pl.ds(y, 8), pl.ds(z, 128)], held.at[i], sems.at[i])
+        slot = lax.rem(i, slots)
+        return pltpu.make_async_copy(x_ref.at[:, pl.ds(y, 8), pl.ds(z, 128)], held.at[slot], sems.at[slot])
 
     @pl.when(step == 0)
     def _():
-        for i in range(steps):
+        for i in range(slots):
             load(i).start()
 
     load(step).wait()
-
-    def fold(t, carry):
-        for j in range(32):
-            i = t * 32 + j
-            near, far = held[step, i], held[step, 2 * half - 1 - i]
-            sums[pl.ds(pl.multiple_of(i * 8, 8), 8), :] = near + far
-            diffs[pl.ds(pl.multiple_of(i * 8, 8), 8), :] = near - far
-        return carry
-
-    lax.fori_loop(0, half // 32, fold, 0)
-    even = even_ref[...]
-    odd = jnp.concatenate([odd_ref[me ^ k] for k in range(DEEP)], axis=0)
+    even = even_ref[...].reshape(half, half)
+    odd = jnp.concatenate([odd_ref[h, me ^ k] for h in range(2) for k in range(DEEP)], axis=0)
     a_rows = a_ref.reshape(half // 2 * 8, 128)
     b_rows = [b.reshape(NORTH * 8, 128) for b in b_refs]
+    rows = held.reshape(slots * half * 2 * 8, 128)
+    base = lax.rem(step, slots) * half * 2 * 8
+
     for y in range(0, 8, 2):
-        s = jnp.concatenate([sums[pl.ds(y + j, half, stride=8), :] for j in range(2)], axis=1)
-        e = dot(even, tall(s))
-        t = jnp.concatenate([diffs[pl.ds(y + j, half, stride=8), :] for j in range(2)], axis=1)
-        o = dot(odd, tall(t))
+        near, far = (
+            jnp.concatenate(
+                [rows[pl.ds(base + first * half * 8 + y + j, half, stride=8), :] for j in range(2)], axis=1
+            )
+            for first in range(2)
+        )
+        far = upside_down(far)
+        e = product(even, near + far)
+        o = product(odd, near - far)
         for j in range(2):
-            a_rows[pl.ds(y + j, half // 2, stride=8), :] = e[:, j * 128 : (j + 1) * 128]
+            lanes = slice(j * 128, j * 128 + 128)
+            a_rows[pl.ds(y + j, half // 2, stride=8), :] = e[:, lanes]
             for k in range(DEEP):
-                b_rows[k][pl.ds(y + j, NORTH, stride=8), :] = o[k * NORTH : (k + 1) * NORTH, j * 128 : (j + 1) * 128]
+                b_rows[k][pl.ds(y + j, NORTH, stride=8), :] = o[k * NORTH : (k + 1) * NORTH, lanes]
+
+    @pl.when(step + slots < steps)
+    def _():
+        load(step + slots).start()
 
 
 def x_stage(source):
@@ -98,9 +115,9 @@
     modes = nx // 2
     block = modes // NORTH
     near = np.arange(nx // 2)
-    even = wide(sines(near, np.arange(0, modes, 2), nx).T)
+    even = np.stack(halves(sines(near, np.arange(0, modes, 2), nx).T))
     odd_modes = (block * np.arange(NORTH)[None, :] + 2 * np.arange(DEEP)[:, None] + 1).reshape(-1)
-    odd = wide(sines(near, odd_modes, nx).T).reshape(DEEP, NORTH, -1)
+    odd = np.stack(halves(sines(near, odd_modes, nx).T)).reshape(2, DEEP, NORTH, -1)
     across = nz // 128
     steps = ny // 8 * across
     b_shape = jax.ShapeDtypeStruct((NORTH, ny, nz), F32)
@@ -111,8 +128,7 @@
         in_specs=[vmem(), vmem(), pl.BlockSpec(memory_space=pl.ANY)],
         out_specs=[pl.BlockSpec((modes // 2, 8, 128), lambda i: (0, i // across, i % across))] + [b_spec] * DEEP,
         out_shape=[jax.ShapeDtypeStruct((modes // 2, ny, nz), F32)] + [b_shape] * DEEP,
-        scratch_shapes=[pltpu.VMEM((nx // 2 * 8, 128), F32)] * 2
-        + [pltpu.VMEM((steps, nx, 8, 128), F32), pltpu.SemaphoreType.DMA((steps,))],
+        scratch_shapes=[pltpu.VMEM((4, nx, 8, 128), F32), pltpu.SemaphoreType.DMA((4,))],
         cost_estimate=cost(6 * nx * modes * ny * nz // 2, 6 * nx * ny * nz),
         name="x_stage",
     )(jnp.asarray(even), jnp.asarray(odd), source)
@@ -122,27 +138,39 @@
     return jnp.asarray(wide(sines(np.arange(ny), np.arange(ny // 2), ny).T).reshape(DEEP, ny // 2 // DEEP, -1))
 
 
-def ya_kernel(table_ref, v_ref, *outs):
-    me = lax.axis_index("deep")
+def ya_kernel(table_ref, v_ref, *refs):
+    outs, (held, sems) = refs[:DEEP], refs[DEEP:]
+    me, j = lax.axis_index("deep"), pl.program_id(0)
+
+    def load(i):
+        return pltpu.make_async_copy(v_ref.at[:, i], held.at[i], sems.at[i])
+
+    @pl.when(j == 0)
+    def _():
+        for i in range(held.shape[0]):
+            load(i).start()
+
+    load(j).wait()
     table = jnp.concatenate([table_ref[me ^ k] for k in range(DEEP)], axis=0)
-    v = v_ref[...]
-    n, _, y, z = v.shape
-    r = dot(table, tall(v.reshape(n * y, z)))
-    m = r.shape[0] // DEEP
-    for k in range(DEEP):
-        outs[k][0] = r[k * m : (k + 1) * m]
+    n, y, z = held.shape[1:]
+    m, block = table.shape[0] // DEEP, 256
+    for i in range(z // block):
+        at = slice(i * block, (i + 1) * block)
+        r = dot(table, tall(held[j, :, :, at].reshape(n * y, block)))
+        for k in range(DEEP):
+            outs[k][0, :, at] = r[k * m : (k + 1) * m]
 
 
 def ya_stage(table, v):
     n, js, y, nz = v.shape
     m = table.shape[1]
-    zb = 256
     return pl.pallas_call(
         ya_kernel,
-        grid=(js, nz // zb),
-        in_specs=[vmem(), pl.BlockSpec((n, 1, y, zb), lambda j, z: (0, j, 0, z))],
-        out_specs=[pl.BlockSpec((1, m, zb), lambda j, z: (j, 0, z))] * DEEP,
+        grid=(js,),
+        in_specs=[vmem(), pl.BlockSpec(memory_space=pltpu.HBM)],
+        out_specs=[pl.BlockSpec((1, m, nz), lambda j: (j, 0, 0))] * DEEP,
         out_shape=[jax.ShapeDtypeStruct((js, m, nz), F32)] * DEEP,
+        scratch_shapes=[pltpu.VMEM((js, n, y, nz), F32), pltpu.SemaphoreType.DMA((js,))],
         cost_estimate=cost(6 * n * y * m * DEEP * js * nz, 6 * n * js * y * nz),
         compiler_params=LIMIT,
         name="ya_stage",
@@ -178,33 +206,63 @@
     return both
 
 
-def zb_kernel(table_ref, near_ref, far_ref, *rest):
-    n, y, z = near_ref.shape
-    even, odd = z_halves(near_ref[...].reshape(n * y, z), far_ref[...].reshape(n * y, z), table_ref)
-    *before, o_ref = rest
-    half = even.shape[1]
-    even, odd = even.reshape(n, y, half), odd.reshape(n, y, half)
-    if before:
-        even, odd = even + before[0][:, :, :half], odd + before[0][:, :, half:]
-    o_ref[:, :, :half] = even
-    o_ref[:, :, half:] = odd
-
-
-def zb_stage(table, near, far, *before):
+def zb_rows(table_ref, near, far, before, o_ref):
+    n, y, z = near.shape
+    both = z_halves(near.reshape(n * y, z), far.reshape(n * y, z), table_ref)
+    for i in range(o_ref.shape[1]):
+        for p in range(2):
+            r = both[p][:, i * 128 : (i + 1) * 128].reshape(n, y, 128)
+            lanes = slice(p * 128, p * 128 + 128)
+            o_ref[:, i, :, lanes] = r if before is None else r + before[:, i, :, lanes]
+
+
+def zb1_kernel(table_ref, near_ref, far_ref, o_ref):
+    zb_rows(table_ref, near_ref[...], far_ref[...], None, o_ref)
+
+
+def zb2_kernel(table_ref, before_ref, near_ref, far_ref, o_ref, near, far, sems):
+    step = pl.program_id(0)
+    rows = o_ref.shape[0]
+
+    def loads(i):
+        return [
+            pltpu.make_async_copy(ref.at[pl.ds(i * rows, rows)], held.at[pl.ds(i * rows, rows)], sems.at[i, k])
+            for k, (ref, held) in enumerate(((near_ref, near), (far_ref, far)))
+        ]
+
+    @pl.when(step == 0)
+    def _():
+        for i in range(near.shape[0] // rows):
+            for copy in loads(i):
+                copy.start()
+
+    for copy in loads(step):
+        copy.wait()
+    at = pl.ds(step * rows, rows)
+    zb_rows(table_ref, near[at], far[at], before_ref, o_ref)
+
+
+def zb_stage(table, near, far, before=None):
     n, y, z = near.shape
     modes, rows = 2 * table.shape[3], 8
     spec = pl.BlockSpec((rows, y, z), lambda i: (i, 0, 0))
-    wide_spec = pl.BlockSpec((rows, y, modes), lambda i: (i, 0, 0))
-    return pl.pallas_call(
-        zb_kernel,
+    wide_spec = pl.BlockSpec((rows, modes // 256, y, 256), lambda i: (i, 0, 0, 0))
+    hbm = pl.BlockSpec(memory_space=pltpu.HBM)
+    first = before is None
+    shape = (n, modes // 256, y, 256)
+    return pl.pallas_call(
+        zb1_kernel if first else zb2_kernel,
         grid=(n // rows,),
-        in_specs=[vmem(), spec, spec] + [wide_spec] * len(before),
+        in_specs=[vmem(), spec, spec] if first else [vmem(), wide_spec, hbm, hbm],
         out_specs=wide_spec,
-        out_shape=pltpu.HBM((n, y, modes), F32) if before else jax.ShapeDtypeStruct((n, y, modes), F32),
+        out_shape=jax.ShapeDtypeStruct(shape, F32) if first else pltpu.HBM(shape, F32),
+        scratch_shapes=[]
+        if first
+        else [pltpu.VMEM((n, y, z), F32)] * 2 + [pltpu.SemaphoreType.DMA((n // rows, 2))],
         cost_estimate=cost(6 * n * y * z * modes, 8 * n * y * (z + modes)),
         compiler_params=LIMIT,
         name="zb_stage",
-    )(table, near, far, *before)
+    )(*((table, near, far) if first else (table, before, near, far)))
 
 
 def za_kernel(sx_ref, t0_ref, t1_ref, sy_ref, sz_ref, p0, p1, p2, p3, o_ref):
@@ -233,23 +291,23 @@
     )(sx, *tables, sy, sz, *pieces)
 
 
-def yb_kernel(sx_ref, table_ref, sy_ref, sz_ref, even_ref, odd_ref, *outs):
+def yb_kernel(sx_ref, table_ref, sy_ref, sz_ref, v_ref, *outs):
     me = lax.axis_index("deep")
+    n, _, y, block = v_ref.shape
     table = jnp.concatenate([table_ref[me ^ k] for k in range(DEEP)], axis=0)
-    n, y, z = even_ref.shape
-    e = dot(table, tall(even_ref[...].reshape(n * y, z)))
-    o = dot(table, tall(odd_ref[...].reshape(n * y, z)))
+    r = dot(table, tall(v_ref[...].reshape(n * y, block)))
     m = table.shape[0] // DEEP
     sx = sx_ref[lax.axis_index("north") * 2 * DEEP + 2 * me + 1]
     for k in range(DEEP):
-        symbol = sx + jnp.concatenate([sy_ref[me ^ k]] * (2 * z // 128), axis=1) + sz_ref[...]
-        outs[k][...] = shuffled(e[k * m : (k + 1) * m], o[k * m : (k + 1) * m]) * lax.rsqrt(symbol)
+        symbol = sx + jnp.concatenate([sy_ref[me ^ k]] * (block // 128), axis=1) + sz_ref[...]
+        rows = slice(k * m, (k + 1) * m)
+        outs[k][...] = shuffled(r[rows, : block // 2], r[rows, block // 2 :]) * lax.rsqrt(symbol)
 
 
 def yb_stage(sx, table, sy, sz, v):
-    n, y, modes = v.shape
-    m, block = table.shape[1], 512
-    steps = modes // block
+    n, steps, y, block = v.shape
+    m = table.shape[1]
+    modes = steps * block
     return pl.pallas_call(
         yb_kernel,
         grid=(steps,),
@@ -258,15 +316,14 @@
             vmem(),
             vmem(),
             pl.BlockSpec((1, block), lambda i: (0, i)),
-            pl.BlockSpec((n, y, block // 2), lambda i: (0, 0, i)),
-            pl.BlockSpec((n, y, block // 2), lambda i: (0, 0, i + 2)),
+            pl.BlockSpec((n, 1, y, block), lambda i: (0, i, 0, 0)),
         ],
         out_specs=[pl.BlockSpec((m, block), lambda i: (0, i))] * DEEP,
         out_shape=[jax.ShapeDtypeStruct((m, modes), F32)] * DEEP,
         cost_estimate=cost(6 * n * y * m * DEEP * modes, 6 * n * y * modes),
         compiler_params=LIMIT,
         name="yb_stage",
-    )(sx, table, sy, sz, v, v)
+    )(sx, table, sy, sz, v)
 
 
 def join_kernel(whole_ref, p0, p1, p2, p3, o_ref, sems):

time: 139 us -> 136 us (0.978)
  Pallas kernels: 39.3 us -> 33.9 us
  waiting for transfers between devices: 50 us -> 52.8 us
    pallas_call x3, Pallas kernels: 15 us -> 11.8 us  [the longest x2 7.17 us: zb_stage(): pl.pallas_call(zb1_kernel if first else zb2_kernel, grid=(n // rows,), in...]
    pallas_call x1, Pallas kernels: 13.8 us -> 11 us  [x_stage(): pl.pallas_call(x_kernel, grid=(steps,), in_specs=[vmem(), vmem(), pl.Bloc...]
    all_to_all x2, waiting for transfers between devices: 17.3 us -> 20 us  [north_exchange(): return lax.all_to_all(v, 'north', split_axis=0, concat_axis=0, tiled=True)]
  transfers between devices with their start and end apart: 11 -> 11, of which waited for: 6 -> 5; matrix products, arithmetic and copies ran while one was open for 13% -> 13% of each run, Pallas kernels for 18% -> 16%
where the time goes in v1:
time: 136 us; the launch traced here: 135 us
  waiting for transfers between devices  52.8 us (39%)
  Pallas kernels  33.9 us (25%)
  starting transfers between devices  29.9 us (22%)
  other arithmetic  17.6 us (13%)
    ppermute x9, waiting for transfers between devices, deep_exchange(): got[k] = lax.ppermute(pieces[k], 'deep', [(s, s ^ k) for s in range(DEEP)])  32.7 us
    all_to_all x2, waiting for transfers between devices, north_exchange(): return lax.all_to_all(v, 'north', split_axis=0, concat_axis=0, tiled=True)  20 us
    all_to_all x2, starting transfers between devices, north_exchange(): return lax.all_to_all(v, 'north', split_axis=0, concat_axis=0, tiled=True)  18 us
    another operation x1, other arithmetic  17.2 us
    ppermute x9, starting transfers between devices, deep_exchange(): got[k] = lax.ppermute(pieces[k], 'deep', [(s, s ^ k) for s in range(DEEP)])  11.9 us
    pallas_call x1, Pallas kernels, x_stage(): pl.pallas_call(x_kernel, grid=(steps,), in_specs=[vmem(), vmem(), pl.Bloc...  11 us
    pallas_call x2, Pallas kernels, zb_stage(): pl.pallas_call(zb1_kernel if first else zb2_kernel, grid=(n // rows,), in...  7.17 us
    pallas_call x1, Pallas kernels, za_stage(): pl.pallas_call(za_kernel, grid=(js,), in_specs=[pl.BlockSpec(memory_space...  5.95 us
  transfers between devices with their start and end apart: 11, of which 5 were waited for; matrix products, arithmetic and copies ran while one was open for 13% of the time, Pallas kernels for 16%

profile of v1, /device:TPU:1, one launch (start us, length us, event | category | flops | bytes accessed | tf_op | source)
XLA Modules:
  0.0 134.7 jit_solution(11715291423806661119)
XLA Ops:
  0.0 11.0 %x_stage.1 = (f32[128,16,512]{2,1,0:T(8,128)}, f32[32,16,512]{2,1,0:T(8,128)}, f32[32,16,512]{2,1,0:T(8,128)}, f32[32,16,512]{2,1,0:T(8,128)}, f32[32,16,512]{2,1,0:T(8,128)}) custom-call(bf16[2,128,256]{2,1,0:T(8,128)(2,1)} %constant.37.clone.even_ref, bf16[2,4,32,256]{3,2,1,0:T(8,128)(2,1)} %constant.38.clone.odd_ref, f32[512,16,512]{2,1,0:T(8,128)} %x_ref.1), custom_call_target="tpu_custom_call" | custom-call | flops 3221225472 | bytes 25165824 | tf_op jit(solution)/shard_map/x_stage/pallas_call | solution.py:125
  11.0 9.5 %all-to-all-start = ((f32[32,4,16,512]{3,2,1,0:T(8,128)}), f32[32,4,16,512]{3,2,1,0:T(8,128)}, u32[]{:S(2)}, u32[]{:S(2)}) async-start(f32[32,4,16,512]{3,2,1,0:T(8,128)} %bitcast.5), calls=%async_computation | async-start | bytes 8388608 | tf_op jit(solution)/shard_map/all_to_all | solution.py:372
  20.5 2.8 %collective-permute-start.3 = (f32[32,16,512]{2,1,0:T(8,128)}, f32[32,16,512]{2,1,0:T(8,128)S(1)}, u32[]{:S(2)}, u32[]{:S(2)}) collective-permute-start(f32[32,16,512]{2,1,0:T(8,128)} %get-tuple-element.24), channel_id=1, source_target_pairs={{0,3},{1,2},{2,1},{3,0},{4,7},{5,6},{6,5},{7,4},{8,11},{9,10},{10,... | collective-permute-start | bytes 3145736 | tf_op jit(solution)/shard_map/ppermute | solution.py:367
  23.3 0.0 collective-permute-start.4
  23.3 1.3 collective-permute-start.5
  24.6 17.2 %reduce-precision_convert_fusion = (bf16[2,1,512,512]{3,2,1,0:T(8,128)(2,1)S(1)}, bf16[2,1,512,512]{3,2,1,0:T(8,128)(2,1)S(1)}, bf16[2,1,512,512]{3,2,1,0:T(8,128)(2,1)S(1)}, bf16[2,1,512,512]{3,2,1,0:T(8,128)(2,1)S(1)}) fusion(s32[512]{0:T(512)S(1)} %get-tuple-element.37, s32[2,512]{1,0:T(2,128)S(1)} %add_add_fusion, s32[512]{0:T(512)S(1)} %get-tuple-element.38), kind=kLoop, calls=%fused_computation.3 | loop fusion | flops 14680064 | bytes 4202496 | tf_op jit(solution)/shard_map/convert
  41.8 0.2 pad_maximum_fusion.1.t1_ref.table_ref
  42.0 0.0 copy-start
  42.0 0.0 copy-start.2
  42.0 0.2 pad_maximum_fusion.t0_ref.table_ref
  42.3 4.3 %collective-permute-done.3.far_ref = f32[32,16,512]{2,1,0:T(8,128)S(1)} collective-permute-done((f32[32,16,512]{2,1,0:T(8,128)}, f32[32,16,512]{2,1,0:T(8,128)S(1)}, u32[]{:S(2)}, u32[]{:S(2)}) %collective-permute-start.3) | collective-permute-done | bytes 1048608 | tf_op jit(solution)/shard_map/ppermute | solution.py:367
  46.6 0.0 copy-done.2
  46.6 2.5 %zb_stage.2.before_ref = f32[32,4,16,256]{3,2,1,0:T(8,128)S(1)} custom-call(bf16[2,2,512,512]{3,2,1,0:T(8,128)(2,1)S(1)} %pad_maximum_fusion.t0_ref.table_ref, f32[32,16,512]{2,1,0:T(8,128)S(1)} %copy-done.2, f32[32,16,512]{2,1,0:T(8,128)S(1)} %collective-permute-done.3.far_ref), custom_call_target="tpu_custom_call" | custom-call | flops 1610612736 | bytes 6291456 | tf_op jit(solution)/shard_map/zb_stage/pallas_call | solution.py:253
  49.1 0.0 collective-permute-done.4.near_ref
  49.1 21.0 %collective-permute-done.5.far_ref = f32[32,16,512]{2,1,0:T(8,128)} collective-permute-done((f32[32,16,512]{2,1,0:T(8,128)}, f32[32,16,512]{2,1,0:T(8,128)}, u32[]{:S(2)}, u32[]{:S(2)}) %collective-permute-start.5) | collective-permute-done | bytes 1048608 | tf_op jit(solution)/shard_map/ppermute | solution.py:367
  70.1 0.0 copy-done
  70.2 4.7 %zb_stage.3 = f32[32,4,16,256]{3,2,1,0:T(8,128)} custom-call(bf16[2,2,512,512]{3,2,1,0:T(8,128)(2,1)S(1)} %pad_maximum_fusion.1.t1_ref.table_ref, f32[32,4,16,256]{3,2,1,0:T(8,128)S(1)} %zb_stage.2.before_ref, f32[32,16,512]{2,1,0:T(8,128)} %collective-permute-done.4.near_ref, f32[32,16,512]{2,1,0:T(8,128)} %collective-permute-done.5.far_ref), custom_call_target="tpu_custom_call" | custom-call | flops 1610612736 | bytes 6291456 | tf_op jit(solution)/shard_map/zb_stage/pallas_call | solution.py:253
  74.8 0.0 copy-start.3
  74.8 0.0 all-to-all-done.v_ref
  74.8 8.5 %all-to-all-start.1 = ((f32[32,4,16,256]{3,2,1,0:T(8,128)}), f32[32,4,16,256]{3,2,1,0:T(8,128)}, u32[]{:S(2)}, u32[]{:S(2)}) async-start(f32[32,4,16,256]{3,2,1,0:T(8,128)} %zb_stage.3), calls=%async_computation.1 | async-start | bytes 4194304 | tf_op jit(solution)/shard_map/all_to_all | solution.py:372
  83.3 0.0 copy-done.3
  83.4 0.0 slice-start
  83.4 0.0 copy-start.5
  83.4 0.0 copy-start.4
  83.4 4.6 %ya_stage.1 = (f32[4,64,512]{2,1,0:T(8,128)S(1)}, f32[4,64,512]{2,1,0:T(8,128)}, f32[4,64,512]{2,1,0:T(8,128)}, f32[4,64,512]{2,1,0:T(8,128)}) custom-call(bf16[4,64,1536]{2,1,0:T(8,128)(2,1)S(1)} %copy-done.3, f32[32,4,16,512]{3,2,1,0:T(8,128)} %all-to-all-done.v_ref), custom_call_target="tpu_custom_call" | custom-call | flops 1610612736 | bytes 6291456 | tf_op jit(solution)/shard_map/ya_stage/pallas_call | solution.py:167
  88.0 0.1 collective-permute-start
  88.1 3.7 %collective-permute-start.1 = (f32[4,64,512]{2,1,0:T(8,128)}, f32[4,64,512]{2,1,0:T(8,128)}, u32[]{:S(2)}, u32[]{:S(2)}) collective-permute-start(f32[4,64,512]{2,1,0:T(8,128)} %get-tuple-element.21), channel_id=1, source_target_pairs={{0,2},{1,3},{2,0},{3,1},{4,6},{5,7},{6,4},{7,5},{8,10},{9,11},{10,... | collective-permute-start | bytes 1572872 | tf_op jit(solution)/shard_map/ppermute | solution.py:367
  91.9 0.1 collective-permute-start.2
  92.0 0.0 slice-done
  92.0 0.1 broadcast_in_dim.6
  92.0 0.0 copy-done.5
  92.0 20.0 %all-to-all-done.1.v_ref = f32[32,4,16,256]{3,2,1,0:T(8,128)} async-done(((f32[32,4,16,256]{3,2,1,0:T(8,128)}), f32[32,4,16,256]{3,2,1,0:T(8,128)}, u32[]{:S(2)}, u32[]{:S(2)}) %all-to-all-start.1) | async-done | bytes 2097184 | tf_op jit(solution)/shard_map/all_to_all | solution.py:372
  112.1 0.0 copy-start.1
  112.1 0.1 broadcast_in_dim.7.sy_ref
  112.2 0.0 copy-done.4
  112.2 4.2 %yb_stage.1 = (f32[64,1024]{1,0:T(8,128)S(1)}, f32[64,1024]{1,0:T(8,128)S(1)}, f32[64,1024]{1,0:T(8,128)S(1)}, f32[64,1024]{1,0:T(8,128)S(1)}) custom-call(f32[512]{0:T(512)S(1)} %copy-done.4, bf16[4,64,1536]{2,1,0:T(8,128)(2,1)S(1)} %copy-done.3, f32[4,64,128]{2,1,0:T(8,128)S(1)} %broadcast_in_dim.7.sy_ref, f32[1,1024]{1,0:T(1,128)S(1)} %bitcast.3, ...), custom_call_target="tpu_custom_call" | custom-call | flops 805306368 | bytes 3145728 | tf_op jit(solution)/shard_map/yb_stage/pallas_call | solution.py:311
  116.4 0.1 collective-permute-start.6
  116.5 3.7 %collective-permute-start.7 = (f32[64,1024]{1,0:T(8,128)S(1)}, f32[64,1024]{1,0:T(8,128)S(1)}, u32[]{:S(2)}, u32[]{:S(2)}) collective-permute-start(f32[64,1024]{1,0:T(8,128)S(1)} %get-tuple-element.29), channel_id=1, source_target_pairs={{0,2},{1,3},{2,0},{3,1},{4,6},{5,7},{6,4},{7,5},{8,10},{9,11},{10,... | collective-permute-start | bytes 786440 | tf_op jit(solution)/shard_map/ppermute | solution.py:367
  120.3 0.0 collective-permute-done.p1
  120.3 0.1 collective-permute-start.8
  120.4 0.0 collective-permute-done.1.p2
  120.4 0.0 collective-permute-done.2.p3
  120.4 0.0 copy-done.1
  120.4 6.0 %za_stage.1.whole_ref = f32[4,2,64,1024]{3,2,1,0:T(8,128)} custom-call(f32[512]{0:T(512)S(1)} %copy-done.4, bf16[2,2,512,512]{3,2,1,0:T(8,128)(2,1)S(1)} %pad_maximum_fusion.t0_ref.table_ref, bf16[2,2,512,512]{3,2,1,0:T(8,128)(2,1)S(1)} %copy-done.1, f32[4,64,128]{2,1,0:T(8,128)S(1)} %broadcast_in_dim.7.sy_ref, f32[1,1024]{1,0:T(1,128)S(1)} %bitcast.4, ...), custom_call_target="tpu_custom_call" | custom-call | flops 1610612736 | bytes 6291456 | tf_op jit(solution)/shard_map/za_stage/pallas_call | solution.py:282
  126.3 0.0 collective-permute-done.6.p1
  126.3 4.4 %collective-permute-done.7.p2 = f32[64,1024]{1,0:T(8,128)S(1)} collective-permute-done((f32[64,1024]{1,0:T(8,128)S(1)}, f32[64,1024]{1,0:T(8,128)S(1)}, u32[]{:S(2)}, u32[]{:S(2)}) %collective-permute-start.7) | collective-permute-done | bytes 262176 | tf_op jit(solution)/shard_map/ppermute | solution.py:367
  130.7 3.0 %collective-permute-done.8.p3 = f32[64,1024]{1,0:T(8,128)S(1)} collective-permute-done((f32[64,1024]{1,0:T(8,128)S(1)}, f32[64,1024]{1,0:T(8,128)S(1)}, u32[]{:S(2)}, u32[]{:S(2)}) %collective-permute-start.8) | collective-permute-done | bytes 262176 | tf_op jit(solution)/shard_map/ppermute | solution.py:367
  133.7 1.0 join_stage.1
  (4 shorter events, 0.0 us)
Async XLA Ops:
  11.0 63.9 %all-to-all-start = ((f32[32,4,16,512]{3,2,1,0:T(8,128)}), f32[32,4,16,512]{3,2,1,0:T(8,128)}, u32[]{:S(2)}, u32[]{:S(2)}) async-start(f32[32,4,16,512]{3,2,1,0:T(8,128)} %bitcast.5), calls=%async_computation | async-start | bytes 8388608 | tf_op jit(solution)/shard_map/all_to_all | solution.py:372
  20.5 26.1 %collective-permute-start.3 = (f32[32,16,512]{2,1,0:T(8,128)}, f32[32,16,512]{2,1,0:T(8,128)S(1)}, u32[]{:S(2)}, u32[]{:S(2)}) collective-permute-start(f32[32,16,512]{2,1,0:T(8,128)} %get-tuple-element.24), channel_id=1, source_target_pairs={{0,3},{1,2},{2,1},{3,0},{4,7},{5,6},{6,5},{7,4},{8,11},{9,10},{10,... | collective-permute-start | bytes 3145736 | tf_op jit(solution)/shard_map/ppermute | solution.py:367
  23.3 25.8 %collective-permute-start.4 = (f32[32,16,512]{2,1,0:T(8,128)}, f32[32,16,512]{2,1,0:T(8,128)}, u32[]{:S(2)}, u32[]{:S(2)}) collective-permute-start(f32[32,16,512]{2,1,0:T(8,128)} %get-tuple-element.25), channel_id=1, source_target_pairs={{0,1},{1,0},{2,3},{3,2},{4,5},{5,4},{6,7},{7,6},{8,9},{9,8},{10,11... | collective-permute-start | bytes 3145736 | tf_op jit(solution)/shard_map/ppermute | solution.py:367
  23.3 46.9 %collective-permute-start.5 = (f32[32,16,512]{2,1,0:T(8,128)}, f32[32,16,512]{2,1,0:T(8,128)}, u32[]{:S(2)}, u32[]{:S(2)}) collective-permute-start(f32[32,16,512]{2,1,0:T(8,128)} %get-tuple-element.26), channel_id=1, source_target_pairs={{0,2},{1,3},{2,0},{3,1},{4,6},{5,7},{6,4},{7,5},{8,10},{9,11},{10,... | collective-permute-start | bytes 3145736 | tf_op jit(solution)/shard_map/ppermute | solution.py:367
  42.0 28.1 %copy-start = (bf16[2,2,512,512]{3,2,1,0:T(8,128)(2,1)}, bf16[2,2,512,512]{3,2,1,0:T(8,128)(2,1)S(1)}, u32[]{:S(2)}) copy-start(bf16[2,2,512,512]{3,2,1,0:T(8,128)(2,1)S(1)} %pad_maximum_fusion.1.t1_ref.table_ref) | copy-start | bytes 6291460
  42.0 4.6 %copy-start.2 = (f32[32,16,512]{2,1,0:T(8,128)S(1)}, f32[32,16,512]{2,1,0:T(8,128)}, u32[]{:S(2)}) copy-start(f32[32,16,512]{2,1,0:T(8,128)} %get-tuple-element.23.near_ref) | copy-start | bytes 3145732
  74.8 8.5 %copy-start.3 = (bf16[4,64,1536]{2,1,0:T(8,128)(2,1)S(1)}, bf16[4,64,1536]{2,1,0:T(8,128)(2,1)}, u32[]{:S(2)}) copy-start(bf16[4,64,1536]{2,1,0:T(8,128)(2,1)} %constant.39.clone.table_ref) | copy-start | bytes 2359300
  74.8 37.2 %all-to-all-start.1 = ((f32[32,4,16,256]{3,2,1,0:T(8,128)}), f32[32,4,16,256]{3,2,1,0:T(8,128)}, u32[]{:S(2)}, u32[]{:S(2)}) async-start(f32[32,4,16,256]{3,2,1,0:T(8,128)} %zb_stage.3), calls=%async_computation.1 | async-start | bytes 4194304 | tf_op jit(solution)/shard_map/all_to_all | solution.py:372
  83.4 8.6 %slice-start = ((f32[512]{0:T(512)}), f32[256]{0:T(256)S(1)}, s32[]{:S(2)}) async-start(f32[512]{0:T(512)} %param.9), calls=%async_computation.2 | async-start | bytes 2048 | tf_op jit(solution)/shard_map/slice | solution.py:382
  83.4 8.7 %copy-start.5 = (f32[2048]{0:T(1024)S(1)}, f32[2048]{0:T(1024)}, u32[]{:S(2)}) copy-start(f32[2048]{0:T(1024)} %param.10) | copy-start | bytes 24580
  83.4 28.8 %copy-start.4 = (f32[512]{0:T(512)S(1)}, f32[512]{0:T(512)}, u32[]{:S(2)}) copy-start(f32[512]{0:T(512)} %sx_ref.3) | copy-start | bytes 6148
  88.0 32.3 %collective-permute-start = (f32[4,64,512]{2,1,0:T(8,128)}, f32[4,64,512]{2,1,0:T(8,128)}, u32[]{:S(2)}, u32[]{:S(2)}) collective-permute-start(f32[4,64,512]{2,1,0:T(8,128)} %get-tuple-element.20), channel_id=1, source_target_pairs={{0,1},{1,0},{2,3},{3,2},{4,5},{5,4},{6,7},{7,6},{8,9},{9,8},{10,11... | collective-permute-start | bytes 1572872 | tf_op jit(solution)/shard_map/ppermute | solution.py:367
  88.1 32.3 %collective-permute-start.1 = (f32[4,64,512]{2,1,0:T(8,128)}, f32[4,64,512]{2,1,0:T(8,128)}, u32[]{:S(2)}, u32[]{:S(2)}) collective-permute-start(f32[4,64,512]{2,1,0:T(8,128)} %get-tuple-element.21), channel_id=1, source_target_pairs={{0,2},{1,3},{2,0},{3,1},{4,6},{5,7},{6,4},{7,5},{8,10},{9,11},{10,... | collective-permute-start | bytes 1572872 | tf_op jit(solution)/shard_map/ppermute | solution.py:367
  91.9 28.5 %collective-permute-start.2 = (f32[4,64,512]{2,1,0:T(8,128)}, f32[4,64,512]{2,1,0:T(8,128)}, u32[]{:S(2)}, u32[]{:S(2)}) collective-permute-start(f32[4,64,512]{2,1,0:T(8,128)} %get-tuple-element.22), channel_id=1, source_target_pairs={{0,3},{1,2},{2,1},{3,0},{4,7},{5,6},{6,5},{7,4},{8,11},{9,10},{10,... | collective-permute-start | bytes 1572872 | tf_op jit(solution)/shard_map/ppermute | solution.py:367
  112.1 8.3 %copy-start.1 = (bf16[2,2,512,512]{3,2,1,0:T(8,128)(2,1)S(1)}, bf16[2,2,512,512]{3,2,1,0:T(8,128)(2,1)}, u32[]{:S(2)}) copy-start(bf16[2,2,512,512]{3,2,1,0:T(8,128)(2,1)} %copy-done) | copy-start | bytes 6291460
  116.4 9.9 %collective-permute-start.6 = (f32[64,1024]{1,0:T(8,128)S(1)}, f32[64,1024]{1,0:T(8,128)S(1)}, u32[]{:S(2)}, u32[]{:S(2)}) collective-permute-start(f32[64,1024]{1,0:T(8,128)S(1)} %get-tuple-element.28), channel_id=1, source_target_pairs={{0,1},{1,0},{2,3},{3,2},{4,5},{5,4},{6,7},{7,6},{8,9},{9,8},{10,11... | collective-permute-start | bytes 786440 | tf_op jit(solution)/shard_map/ppermute | solution.py:367
  116.5 14.2 %collective-permute-start.7 = (f32[64,1024]{1,0:T(8,128)S(1)}, f32[64,1024]{1,0:T(8,128)S(1)}, u32[]{:S(2)}, u32[]{:S(2)}) collective-permute-start(f32[64,1024]{1,0:T(8,128)S(1)} %get-tuple-element.29), channel_id=1, source_target_pairs={{0,2},{1,3},{2,0},{3,1},{4,6},{5,7},{6,4},{7,5},{8,10},{9,11},{10,... | collective-permute-start | bytes 786440 | tf_op jit(solution)/shard_map/ppermute | solution.py:367
  120.3 13.4 %collective-permute-start.8 = (f32[64,1024]{1,0:T(8,128)S(1)}, f32[64,1024]{1,0:T(8,128)S(1)}, u32[]{:S(2)}, u32[]{:S(2)}) collective-permute-start(f32[64,1024]{1,0:T(8,128)S(1)} %get-tuple-element.30), channel_id=1, source_target_pairs={{0,3},{1,2},{2,1},{3,0},{4,7},{5,6},{6,5},{7,4},{8,11},{9,10},{10,... | collective-permute-start | bytes 786440 | tf_op jit(solution)/shard_map/ppermute | solution.py:367

commit v2 on v1

--- a/solution.py
+++ b/solution.py
@@ -293,21 +293,23 @@
 
 def yb_kernel(sx_ref, table_ref, sy_ref, sz_ref, v_ref, *outs):
     me = lax.axis_index("deep")
-    n, _, y, block = v_ref.shape
+    n, blocks, y, block = v_ref.shape
     table = jnp.concatenate([table_ref[me ^ k] for k in range(DEEP)], axis=0)
-    r = dot(table, tall(v_ref[...].reshape(n * y, block)))
     m = table.shape[0] // DEEP
     sx = sx_ref[lax.axis_index("north") * 2 * DEEP + 2 * me + 1]
-    for k in range(DEEP):
-        symbol = sx + jnp.concatenate([sy_ref[me ^ k]] * (block // 128), axis=1) + sz_ref[...]
-        rows = slice(k * m, (k + 1) * m)
-        outs[k][...] = shuffled(r[rows, : block // 2], r[rows, block // 2 :]) * lax.rsqrt(symbol)
+    for b in range(blocks):
+        r = dot(table, tall(v_ref[:, b].reshape(n * y, block)))
+        lanes = slice(b * block, (b + 1) * block)
+        for k in range(DEEP):
+            symbol = sx + jnp.concatenate([sy_ref[me ^ k]] * (block // 128), axis=1) + sz_ref[:, lanes]
+            rows = slice(k * m, (k + 1) * m)
+            outs[k][:, lanes] = shuffled(r[rows, : block // 2], r[rows, block // 2 :]) * lax.rsqrt(symbol)
 
 
 def yb_stage(sx, table, sy, sz, v):
-    n, steps, y, block = v.shape
+    n, blocks, y, block = v.shape
     m = table.shape[1]
-    modes = steps * block
+    modes, steps = blocks * block, 2
     return pl.pallas_call(
         yb_kernel,
         grid=(steps,),
@@ -315,10 +317,10 @@
             pl.BlockSpec(memory_space=pltpu.SMEM),
             vmem(),
             vmem(),
-            pl.BlockSpec((1, block), lambda i: (0, i)),
-            pl.BlockSpec((n, 1, y, block), lambda i: (0, i, 0, 0)),
+            pl.BlockSpec((1, modes // steps), lambda i: (0, i)),
+            pl.BlockSpec((n, blocks // steps, y, block), lambda i: (0, i, 0, 0)),
         ],
-        out_specs=[pl.BlockSpec((m, block), lambda i: (0, i))] * DEEP,
+        out_specs=[pl.BlockSpec((m, modes // steps), lambda i: (0, i))] * DEEP,
         out_shape=[jax.ShapeDtypeStruct((m, modes), F32)] * DEEP,
         cost_estimate=cost(6 * n * y * m * DEEP * modes, 6 * n * y * modes),
         compiler_params=LIMIT,

time: 136 us -> 135 us (level)
  no operation moved by 1% of the time
where the time goes in v2:
time: 135 us; the launch traced here: 134 us
  waiting for transfers between devices  52.8 us (39%)
  Pallas kernels  33.1 us (25%)
  starting transfers between devices  29.9 us (22%)
  other arithmetic  17.6 us (13%)
    ppermute x9, waiting for transfers between devices, deep_exchange(): got[k] = lax.ppermute(pieces[k], 'deep', [(s, s ^ k) for s in range(DEEP)])  32.7 us
    all_to_all x2, waiting for transfers between devices, north_exchange(): return lax.all_to_all(v, 'north', split_axis=0, concat_axis=0, tiled=True)  20 us
    all_to_all x2, starting transfers between devices, north_exchange(): return lax.all_to_all(v, 'north', split_axis=0, concat_axis=0, tiled=True)  18 us
    another operation x1, other arithmetic  17.2 us
    ppermute x9, starting transfers between devices, deep_exchange(): got[k] = lax.ppermute(pieces[k], 'deep', [(s, s ^ k) for s in range(DEEP)])  11.9 us
    pallas_call x1, Pallas kernels, x_stage(): pl.pallas_call(x_kernel, grid=(steps,), in_specs=[vmem(), vmem(), pl.Bloc...  11 us
    pallas_call x2, Pallas kernels, zb_stage(): pl.pallas_call(zb1_kernel if first else zb2_kernel, grid=(n // rows,), in...  7.17 us
    pallas_call x1, Pallas kernels, za_stage(): pl.pallas_call(za_kernel, grid=(js,), in_specs=[pl.BlockSpec(memory_space...  5.96 us
  transfers between devices with their start and end apart: 11, of which 5 were waited for; matrix products, arithmetic and copies ran while one was open for 13% of the time, Pallas kernels for 16%

profile of v2, /device:TPU:1, one launch (start us, length us, event | category | flops | bytes accessed | tf_op | source)
XLA Modules:
  0.0 133.9 jit_solution(5129250198466528778)
XLA Ops:
  0.0 11.0 %x_stage.1 = (f32[128,16,512]{2,1,0:T(8,128)}, f32[32,16,512]{2,1,0:T(8,128)}, f32[32,16,512]{2,1,0:T(8,128)}, f32[32,16,512]{2,1,0:T(8,128)}, f32[32,16,512]{2,1,0:T(8,128)}) custom-call(bf16[2,128,256]{2,1,0:T(8,128)(2,1)} %constant.37.clone.even_ref, bf16[2,4,32,256]{3,2,1,0:T(8,128)(2,1)} %constant.38.clone.odd_ref, f32[512,16,512]{2,1,0:T(8,128)} %x_ref.1), custom_call_target="tpu_custom_call" | custom-call | flops 3221225472 | bytes 25165824 | tf_op jit(solution)/shard_map/x_stage/pallas_call | solution.py:125
  11.0 9.5 %all-to-all-start = ((f32[32,4,16,512]{3,2,1,0:T(8,128)}), f32[32,4,16,512]{3,2,1,0:T(8,128)}, u32[]{:S(2)}, u32[]{:S(2)}) async-start(f32[32,4,16,512]{3,2,1,0:T(8,128)} %bitcast.5), calls=%async_computation | async-start | bytes 8388608 | tf_op jit(solution)/shard_map/all_to_all | solution.py:374
  20.5 2.8 %collective-permute-start.3 = (f32[32,16,512]{2,1,0:T(8,128)}, f32[32,16,512]{2,1,0:T(8,128)S(1)}, u32[]{:S(2)}, u32[]{:S(2)}) collective-permute-start(f32[32,16,512]{2,1,0:T(8,128)} %get-tuple-element.24), channel_id=1, source_target_pairs={{0,3},{1,2},{2,1},{3,0},{4,7},{5,6},{6,5},{7,4},{8,11},{9,10},{10,... | collective-permute-start | bytes 3145736 | tf_op jit(solution)/shard_map/ppermute | solution.py:369
  23.3 0.0 collective-permute-start.4
  23.3 1.3 collective-permute-start.5
  24.6 17.2 %reduce-precision_convert_fusion = (bf16[2,1,512,512]{3,2,1,0:T(8,128)(2,1)S(1)}, bf16[2,1,512,512]{3,2,1,0:T(8,128)(2,1)S(1)}, bf16[2,1,512,512]{3,2,1,0:T(8,128)(2,1)S(1)}, bf16[2,1,512,512]{3,2,1,0:T(8,128)(2,1)S(1)}) fusion(s32[512]{0:T(512)S(1)} %get-tuple-element.37, s32[2,512]{1,0:T(2,128)S(1)} %add_add_fusion, s32[512]{0:T(512)S(1)} %get-tuple-element.38), kind=kLoop, calls=%fused_computation.3 | loop fusion | flops 14680064 | bytes 4202496 | tf_op jit(solution)/shard_map/convert
  41.8 0.2 pad_maximum_fusion.1.t1_ref.table_ref
  42.0 0.0 copy-start
  42.0 0.0 copy-start.2
  42.0 0.2 pad_maximum_fusion.t0_ref.table_ref
  42.3 4.3 %collective-permute-done.3.far_ref = f32[32,16,512]{2,1,0:T(8,128)S(1)} collective-permute-done((f32[32,16,512]{2,1,0:T(8,128)}, f32[32,16,512]{2,1,0:T(8,128)S(1)}, u32[]{:S(2)}, u32[]{:S(2)}) %collective-permute-start.3) | collective-permute-done | bytes 1048608 | tf_op jit(solution)/shard_map/ppermute | solution.py:369
  46.6 0.0 copy-done.2
  46.6 2.5 %zb_stage.2.before_ref = f32[32,4,16,256]{3,2,1,0:T(8,128)S(1)} custom-call(bf16[2,2,512,512]{3,2,1,0:T(8,128)(2,1)S(1)} %pad_maximum_fusion.t0_ref.table_ref, f32[32,16,512]{2,1,0:T(8,128)S(1)} %copy-done.2, f32[32,16,512]{2,1,0:T(8,128)S(1)} %collective-permute-done.3.far_ref), custom_call_target="tpu_custom_call" | custom-call | flops 1610612736 | bytes 6291456 | tf_op jit(solution)/shard_map/zb_stage/pallas_call | solution.py:253
  49.1 0.0 collective-permute-done.4.near_ref
  49.1 21.0 %collective-permute-done.5.far_ref = f32[32,16,512]{2,1,0:T(8,128)} collective-permute-done((f32[32,16,512]{2,1,0:T(8,128)}, f32[32,16,512]{2,1,0:T(8,128)}, u32[]{:S(2)}, u32[]{:S(2)}) %collective-permute-start.5) | collective-permute-done | bytes 1048608 | tf_op jit(solution)/shard_map/ppermute | solution.py:369
  70.1 0.0 copy-done
  70.2 4.7 %zb_stage.3 = f32[32,4,16,256]{3,2,1,0:T(8,128)} custom-call(bf16[2,2,512,512]{3,2,1,0:T(8,128)(2,1)S(1)} %pad_maximum_fusion.1.t1_ref.table_ref, f32[32,4,16,256]{3,2,1,0:T(8,128)S(1)} %zb_stage.2.before_ref, f32[32,16,512]{2,1,0:T(8,128)} %collective-permute-done.4.near_ref, f32[32,16,512]{2,1,0:T(8,128)} %collective-permute-done.5.far_ref), custom_call_target="tpu_custom_call" | custom-call | flops 1610612736 | bytes 6291456 | tf_op jit(solution)/shard_map/zb_stage/pallas_call | solution.py:253
  74.8 0.0 copy-start.3
  74.8 0.0 all-to-all-done.v_ref
  74.8 8.5 %all-to-all-start.1 = ((f32[32,4,16,256]{3,2,1,0:T(8,128)}), f32[32,4,16,256]{3,2,1,0:T(8,128)}, u32[]{:S(2)}, u32[]{:S(2)}) async-start(f32[32,4,16,256]{3,2,1,0:T(8,128)} %zb_stage.3), calls=%async_computation.1 | async-start | bytes 4194304 | tf_op jit(solution)/shard_map/all_to_all | solution.py:374
  83.3 0.0 copy-done.3
  83.4 0.0 slice-start
  83.4 0.0 copy-start.5
  83.4 0.0 copy-start.4
  83.4 4.6 %ya_stage.1 = (f32[4,64,512]{2,1,0:T(8,128)S(1)}, f32[4,64,512]{2,1,0:T(8,128)}, f32[4,64,512]{2,1,0:T(8,128)}, f32[4,64,512]{2,1,0:T(8,128)}) custom-call(bf16[4,64,1536]{2,1,0:T(8,128)(2,1)S(1)} %copy-done.3, f32[32,4,16,512]{3,2,1,0:T(8,128)} %all-to-all-done.v_ref), custom_call_target="tpu_custom_call" | custom-call | flops 1610612736 | bytes 6291456 | tf_op jit(solution)/shard_map/ya_stage/pallas_call | solution.py:167
  88.0 0.1 collective-permute-start
  88.1 3.7 %collective-permute-start.1 = (f32[4,64,512]{2,1,0:T(8,128)}, f32[4,64,512]{2,1,0:T(8,128)}, u32[]{:S(2)}, u32[]{:S(2)}) collective-permute-start(f32[4,64,512]{2,1,0:T(8,128)} %get-tuple-element.21), channel_id=1, source_target_pairs={{0,2},{1,3},{2,0},{3,1},{4,6},{5,7},{6,4},{7,5},{8,10},{9,11},{10,... | collective-permute-start | bytes 1572872 | tf_op jit(solution)/shard_map/ppermute | solution.py:369
  91.9 0.1 collective-permute-start.2
  92.0 0.0 slice-done
  92.0 0.1 broadcast_in_dim.6
  92.0 0.0 copy-done.5
  92.0 20.0 %all-to-all-done.1.v_ref = f32[32,4,16,256]{3,2,1,0:T(8,128)} async-done(((f32[32,4,16,256]{3,2,1,0:T(8,128)}), f32[32,4,16,256]{3,2,1,0:T(8,128)}, u32[]{:S(2)}, u32[]{:S(2)}) %all-to-all-start.1) | async-done | bytes 2097184 | tf_op jit(solution)/shard_map/all_to_all | solution.py:374
  112.1 0.0 copy-start.1
  112.1 0.1 broadcast_in_dim.7.sy_ref
  112.2 0.0 copy-done.4
  112.2 3.5 %yb_stage.1 = (f32[64,1024]{1,0:T(8,128)S(1)}, f32[64,1024]{1,0:T(8,128)S(1)}, f32[64,1024]{1,0:T(8,128)S(1)}, f32[64,1024]{1,0:T(8,128)S(1)}) custom-call(f32[512]{0:T(512)S(1)} %copy-done.4, bf16[4,64,1536]{2,1,0:T(8,128)(2,1)S(1)} %copy-done.3, f32[4,64,128]{2,1,0:T(8,128)S(1)} %broadcast_in_dim.7.sy_ref, f32[1,1024]{1,0:T(1,128)S(1)} %bitcast.3, ...), custom_call_target="tpu_custom_call" | custom-call | flops 805306368 | bytes 3145728 | tf_op jit(solution)/shard_map/yb_stage/pallas_call | solution.py:313
  115.6 0.1 collective-permute-start.6
  115.7 3.8 %collective-permute-start.7 = (f32[64,1024]{1,0:T(8,128)S(1)}, f32[64,1024]{1,0:T(8,128)S(1)}, u32[]{:S(2)}, u32[]{:S(2)}) collective-permute-start(f32[64,1024]{1,0:T(8,128)S(1)} %get-tuple-element.29), channel_id=1, source_target_pairs={{0,2},{1,3},{2,0},{3,1},{4,6},{5,7},{6,4},{7,5},{8,10},{9,11},{10,... | collective-permute-start | bytes 786440 | tf_op jit(solution)/shard_map/ppermute | solution.py:369
  119.5 0.0 collective-permute-done.p1
  119.5 0.1 collective-permute-start.8
  119.6 0.0 collective-permute-done.1.p2
  119.6 0.0 collective-permute-done.2.p3
  119.6 0.0 copy-done.1
  119.6 6.0 %za_stage.1.whole_ref = f32[4,2,64,1024]{3,2,1,0:T(8,128)} custom-call(f32[512]{0:T(512)S(1)} %copy-done.4, bf16[2,2,512,512]{3,2,1,0:T(8,128)(2,1)S(1)} %pad_maximum_fusion.t0_ref.table_ref, bf16[2,2,512,512]{3,2,1,0:T(8,128)(2,1)S(1)} %copy-done.1, f32[4,64,128]{2,1,0:T(8,128)S(1)} %broadcast_in_dim.7.sy_ref, f32[1,1024]{1,0:T(1,128)S(1)} %bitcast.4, ...), custom_call_target="tpu_custom_call" | custom-call | flops 1610612736 | bytes 6291456 | tf_op jit(solution)/shard_map/za_stage/pallas_call | solution.py:282
  125.6 0.0 collective-permute-done.6.p1
  125.6 4.4 %collective-permute-done.7.p2 = f32[64,1024]{1,0:T(8,128)S(1)} collective-permute-done((f32[64,1024]{1,0:T(8,128)S(1)}, f32[64,1024]{1,0:T(8,128)S(1)}, u32[]{:S(2)}, u32[]{:S(2)}) %collective-permute-start.7) | collective-permute-done | bytes 262176 | tf_op jit(solution)/shard_map/ppermute | solution.py:369
  129.9 3.0 %collective-permute-done.8.p3 = f32[64,1024]{1,0:T(8,128)S(1)} collective-permute-done((f32[64,1024]{1,0:T(8,128)S(1)}, f32[64,1024]{1,0:T(8,128)S(1)}, u32[]{:S(2)}, u32[]{:S(2)}) %collective-permute-start.8) | collective-permute-done | bytes 262176 | tf_op jit(solution)/shard_map/ppermute | solution.py:369
  132.9 1.0 join_stage.1
  (4 shorter events, 0.0 us)
Async XLA Ops:
  11.0 63.9 %all-to-all-start = ((f32[32,4,16,512]{3,2,1,0:T(8,128)}), f32[32,4,16,512]{3,2,1,0:T(8,128)}, u32[]{:S(2)}, u32[]{:S(2)}) async-start(f32[32,4,16,512]{3,2,1,0:T(8,128)} %bitcast.5), calls=%async_computation | async-start | bytes 8388608 | tf_op jit(solution)/shard_map/all_to_all | solution.py:374
  20.5 26.1 %collective-permute-start.3 = (f32[32,16,512]{2,1,0:T(8,128)}, f32[32,16,512]{2,1,0:T(8,128)S(1)}, u32[]{:S(2)}, u32[]{:S(2)}) collective-permute-start(f32[32,16,512]{2,1,0:T(8,128)} %get-tuple-element.24), channel_id=1, source_target_pairs={{0,3},{1,2},{2,1},{3,0},{4,7},{5,6},{6,5},{7,4},{8,11},{9,10},{10,... | collective-permute-start | bytes 3145736 | tf_op jit(solution)/shard_map/ppermute | solution.py:369
  23.3 25.8 %collective-permute-start.4 = (f32[32,16,512]{2,1,0:T(8,128)}, f32[32,16,512]{2,1,0:T(8,128)}, u32[]{:S(2)}, u32[]{:S(2)}) collective-permute-start(f32[32,16,512]{2,1,0:T(8,128)} %get-tuple-element.25), channel_id=1, source_target_pairs={{0,1},{1,0},{2,3},{3,2},{4,5},{5,4},{6,7},{7,6},{8,9},{9,8},{10,11... | collective-permute-start | bytes 3145736 | tf_op jit(solution)/shard_map/ppermute | solution.py:369
  23.3 46.9 %collective-permute-start.5 = (f32[32,16,512]{2,1,0:T(8,128)}, f32[32,16,512]{2,1,0:T(8,128)}, u32[]{:S(2)}, u32[]{:S(2)}) collective-permute-start(f32[32,16,512]{2,1,0:T(8,128)} %get-tuple-element.26), channel_id=1, source_target_pairs={{0,2},{1,3},{2,0},{3,1},{4,6},{5,7},{6,4},{7,5},{8,10},{9,11},{10,... | collective-permute-start | bytes 3145736 | tf_op jit(solution)/shard_map/ppermute | solution.py:369
  42.0 28.1 %copy-start = (bf16[2,2,512,512]{3,2,1,0:T(8,128)(2,1)}, bf16[2,2,512,512]{3,2,1,0:T(8,128)(2,1)S(1)}, u32[]{:S(2)}) copy-start(bf16[2,2,512,512]{3,2,1,0:T(8,128)(2,1)S(1)} %pad_maximum_fusion.1.t1_ref.table_ref) | copy-start | bytes 6291460
  42.0 4.6 %copy-start.2 = (f32[32,16,512]{2,1,0:T(8,128)S(1)}, f32[32,16,512]{2,1,0:T(8,128)}, u32[]{:S(2)}) copy-start(f32[32,16,512]{2,1,0:T(8,128)} %get-tuple-element.23.near_ref) | copy-start | bytes 3145732
  74.8 8.5 %copy-start.3 = (bf16[4,64,1536]{2,1,0:T(8,128)(2,1)S(1)}, bf16[4,64,1536]{2,1,0:T(8,128)(2,1)}, u32[]{:S(2)}) copy-start(bf16[4,64,1536]{2,1,0:T(8,128)(2,1)} %constant.39.clone.table_ref) | copy-start | bytes 2359300
  74.8 37.2 %all-to-all-start.1 = ((f32[32,4,16,256]{3,2,1,0:T(8,128)}), f32[32,4,16,256]{3,2,1,0:T(8,128)}, u32[]{:S(2)}, u32[]{:S(2)}) async-start(f32[32,4,16,256]{3,2,1,0:T(8,128)} %zb_stage.3), calls=%async_computation.1 | async-start | bytes 4194304 | tf_op jit(solution)/shard_map/all_to_all | solution.py:374
  83.4 8.6 %slice-start = ((f32[512]{0:T(512)}), f32[256]{0:T(256)S(1)}, s32[]{:S(2)}) async-start(f32[512]{0:T(512)} %param.9), calls=%async_computation.2 | async-start | bytes 2048 | tf_op jit(solution)/shard_map/slice | solution.py:384
  83.4 8.7 %copy-start.5 = (f32[2048]{0:T(1024)S(1)}, f32[2048]{0:T(1024)}, u32[]{:S(2)}) copy-start(f32[2048]{0:T(1024)} %param.10) | copy-start | bytes 24580
  83.4 28.8 %copy-start.4 = (f32[512]{0:T(512)S(1)}, f32[512]{0:T(512)}, u32[]{:S(2)}) copy-start(f32[512]{0:T(512)} %sx_ref.3) | copy-start | bytes 6148
  88.0 31.5 %collective-permute-start = (f32[4,64,512]{2,1,0:T(8,128)}, f32[4,64,512]{2,1,0:T(8,128)}, u32[]{:S(2)}, u32[]{:S(2)}) collective-permute-start(f32[4,64,512]{2,1,0:T(8,128)} %get-tuple-element.20), channel_id=1, source_target_pairs={{0,1},{1,0},{2,3},{3,2},{4,5},{5,4},{6,7},{7,6},{8,9},{9,8},{10,11... | collective-permute-start | bytes 1572872 | tf_op jit(solution)/shard_map/ppermute | solution.py:369
  88.1 31.5 %collective-permute-start.1 = (f32[4,64,512]{2,1,0:T(8,128)}, f32[4,64,512]{2,1,0:T(8,128)}, u32[]{:S(2)}, u32[]{:S(2)}) collective-permute-start(f32[4,64,512]{2,1,0:T(8,128)} %get-tuple-element.21), channel_id=1, source_target_pairs={{0,2},{1,3},{2,0},{3,1},{4,6},{5,7},{6,4},{7,5},{8,10},{9,11},{10,... | collective-permute-start | bytes 1572872 | tf_op jit(solution)/shard_map/ppermute | solution.py:369
  91.9 27.7 %collective-permute-start.2 = (f32[4,64,512]{2,1,0:T(8,128)}, f32[4,64,512]{2,1,0:T(8,128)}, u32[]{:S(2)}, u32[]{:S(2)}) collective-permute-start(f32[4,64,512]{2,1,0:T(8,128)} %get-tuple-element.22), channel_id=1, source_target_pairs={{0,3},{1,2},{2,1},{3,0},{4,7},{5,6},{6,5},{7,4},{8,11},{9,10},{10,... | collective-permute-start | bytes 1572872 | tf_op jit(solution)/shard_map/ppermute | solution.py:369
  112.1 7.5 %copy-start.1 = (bf16[2,2,512,512]{3,2,1,0:T(8,128)(2,1)S(1)}, bf16[2,2,512,512]{3,2,1,0:T(8,128)(2,1)}, u32[]{:S(2)}) copy-start(bf16[2,2,512,512]{3,2,1,0:T(8,128)(2,1)} %copy-done) | copy-start | bytes 6291460
  115.6 9.9 %collective-permute-start.6 = (f32[64,1024]{1,0:T(8,128)S(1)}, f32[64,1024]{1,0:T(8,128)S(1)}, u32[]{:S(2)}, u32[]{:S(2)}) collective-permute-start(f32[64,1024]{1,0:T(8,128)S(1)} %get-tuple-element.28), channel_id=1, source_target_pairs={{0,1},{1,0},{2,3},{3,2},{4,5},{5,4},{6,7},{7,6},{8,9},{9,8},{10,11... | collective-permute-start | bytes 786440 | tf_op jit(solution)/shard_map/ppermute | solution.py:369
  115.7 14.2 %collective-permute-start.7 = (f32[64,1024]{1,0:T(8,128)S(1)}, f32[64,1024]{1,0:T(8,128)S(1)}, u32[]{:S(2)}, u32[]{:S(2)}) collective-permute-start(f32[64,1024]{1,0:T(8,128)S(1)} %get-tuple-element.29), channel_id=1, source_target_pairs={{0,2},{1,3},{2,0},{3,1},{4,6},{5,7},{6,4},{7,5},{8,10},{9,11},{10,... | collective-permute-start | bytes 786440 | tf_op jit(solution)/shard_map/ppermute | solution.py:369
  119.5 13.4 %collective-permute-start.8 = (f32[64,1024]{1,0:T(8,128)S(1)}, f32[64,1024]{1,0:T(8,128)S(1)}, u32[]{:S(2)}, u32[]{:S(2)}) collective-permute-start(f32[64,1024]{1,0:T(8,128)S(1)} %get-tuple-element.30), channel_id=1, source_target_pairs={{0,3},{1,2},{2,1},{3,0},{4,7},{5,6},{6,5},{7,4},{8,11},{9,10},{10,... | collective-permute-start | bytes 786440 | tf_op jit(solution)/shard_map/ppermute | solution.py:369

commit v3 on v2

--- a/solution.py
+++ b/solution.py
@@ -1,3 +1,5 @@
+import functools
+
 import jax
 import jax.numpy as jnp
 import numpy as np
@@ -138,12 +140,12 @@
     return jnp.asarray(wide(sines(np.arange(ny), np.arange(ny // 2), ny).T).reshape(DEEP, ny // 2 // DEEP, -1))
 
 
-def ya_kernel(table_ref, v_ref, *refs):
+def ya_kernel(first, table_ref, v_ref, *refs):
     outs, (held, sems) = refs[:DEEP], refs[DEEP:]
     me, j = lax.axis_index("deep"), pl.program_id(0)
 
     def load(i):
-        return pltpu.make_async_copy(v_ref.at[:, i], held.at[i], sems.at[i])
+        return pltpu.make_async_copy(v_ref.at[:, first + i], held.at[i], sems.at[i])
 
     @pl.when(j == 0)
     def _():
@@ -161,11 +163,11 @@
             outs[k][0, :, at] = r[k * m : (k + 1) * m]
 
 
-def ya_stage(table, v):
-    n, js, y, nz = v.shape
+def ya_stage(table, v, first, js):
+    n, _, y, nz = v.shape
     m = table.shape[1]
     return pl.pallas_call(
-        ya_kernel,
+        functools.partial(ya_kernel, first),
         grid=(js,),
         in_specs=[vmem(), pl.BlockSpec(memory_space=pltpu.HBM)],
         out_specs=[pl.BlockSpec((1, m, nz), lambda j: (j, 0, 0))] * DEEP,
@@ -265,30 +267,35 @@
     )(*((table, near, far) if first else (table, before, near, far)))
 
 
-def za_kernel(sx_ref, t0_ref, t1_ref, sy_ref, sz_ref, p0, p1, p2, p3, o_ref):
+def za_kernel(first, sx_ref, t0_ref, t1_ref, sy_ref, sz_ref, p0, p1, p2, p3, *rest):
+    o_ref = rest[-1]
     m, z = p0.shape[1], p0.shape[2]
     even0, odd0 = z_halves(p0[...].reshape(m, z), p3[...].reshape(m, z), t0_ref)
     even1, odd1 = z_halves(p1[...].reshape(m, z), p2[...].reshape(m, z), t1_ref)
     total = shuffled(even0 + even1, odd0 + odd1)
     yz = jnp.concatenate([sy_ref[lax.axis_index("deep")]] * (o_ref.shape[3] // 128), axis=1) + sz_ref[...]
-    first = lax.axis_index("north") * 2 * pl.num_programs(0)
-    o_ref[0, 0] = total * lax.rsqrt(sx_ref[first + 2 * pl.program_id(0)] + yz)
-
-
-def za_stage(sx, tables, sy, sz, pieces):
+    mode = (lax.axis_index("north") * DEEP + first + pl.program_id(0)) * 2
+    o_ref[0, 0] = total * lax.rsqrt(sx_ref[mode] + yz)
+
+
+def za_stage(sx, tables, sy, sz, pieces, first, *whole):
     js, m, z = pieces[0].shape
     modes = 2 * tables[0].shape[3]
     spec = pl.BlockSpec((1, m, z), lambda j: (j, 0, 0))
     return pl.pallas_call(
-        za_kernel,
+        functools.partial(za_kernel, first),
         grid=(js,),
-        in_specs=[pl.BlockSpec(memory_space=pltpu.SMEM)] + [vmem()] * 4 + [spec] * DEEP,
-        out_specs=pl.BlockSpec((1, 1, m, modes), lambda j: (j, 0, 0, 0)),
-        out_shape=jax.ShapeDtypeStruct((js, 2, m, modes), F32),
+        in_specs=[pl.BlockSpec(memory_space=pltpu.SMEM)]
+        + [vmem()] * 4
+        + [spec] * DEEP
+        + [pl.BlockSpec(memory_space=pl.ANY)] * len(whole),
+        out_specs=pl.BlockSpec((1, 1, m, modes), lambda j: (first + j, 0, 0, 0)),
+        out_shape=jax.ShapeDtypeStruct((DEEP, 2, m, modes), F32),
+        input_output_aliases={5 + DEEP: 0} if whole else {},
         cost_estimate=cost(6 * js * m * z * 2 * modes, 4 * js * m * z * DEEP + 8 * z * modes),
         compiler_params=LIMIT,
         name="za_stage",
-    )(sx, *tables, sy, sz, *pieces)
+    )(sx, *tables, sy, sz, *pieces, *whole)
 
 
 def yb_kernel(sx_ref, table_ref, sy_ref, sz_ref, v_ref, *outs):
@@ -306,21 +313,22 @@
             outs[k][:, lanes] = shuffled(r[rows, : block // 2], r[rows, block // 2 :]) * lax.rsqrt(symbol)
 
 
-def yb_stage(sx, table, sy, sz, v):
+def yb_stage(sx, table, sy, sz, v, part, parts):
     n, blocks, y, block = v.shape
     m = table.shape[1]
-    modes, steps = blocks * block, 2
+    blocks //= parts
+    modes = blocks * block
     return pl.pallas_call(
         yb_kernel,
-        grid=(steps,),
+        grid=(1,),
         in_specs=[
             pl.BlockSpec(memory_space=pltpu.SMEM),
             vmem(),
             vmem(),
-            pl.BlockSpec((1, modes // steps), lambda i: (0, i)),
-            pl.BlockSpec((n, blocks // steps, y, block), lambda i: (0, i, 0, 0)),
+            pl.BlockSpec((1, modes), lambda i: (0, part)),
+            pl.BlockSpec((n, blocks, y, block), lambda i: (0, part, 0, 0)),
         ],
-        out_specs=[pl.BlockSpec((m, modes // steps), lambda i: (0, i))] * DEEP,
+        out_specs=[pl.BlockSpec((m, modes), lambda i: (0, 0))] * DEEP,
         out_shape=[jax.ShapeDtypeStruct((m, modes), F32)] * DEEP,
         cost_estimate=cost(6 * n * y * m * DEEP * modes, 6 * n * y * modes),
         compiler_params=LIMIT,
@@ -328,11 +336,15 @@
     )(sx, table, sy, sz, v)
 
 
-def join_kernel(whole_ref, p0, p1, p2, p3, o_ref, sems):
+def join_kernel(whole_ref, *refs):
+    pieces, (o_ref, sems) = refs[:-2], refs[-2:]
     me = lax.axis_index("deep")
-    copies = [
-        pltpu.make_async_copy(p, o_ref.at[me ^ k, 1], sems.at[k]) for k, p in enumerate((p0, p1, p2, p3))
-    ]
+    copies = []
+    for i, piece in enumerate(pieces):
+        part, k = divmod(i, DEEP)
+        modes = piece.shape[1]
+        place = o_ref.at[me ^ k, 1, :, pl.ds(part * modes, modes)]
+        copies.append(pltpu.make_async_copy(piece, place, sems.at[i]))
     for copy in copies:
         copy.start()
     for copy in copies:
@@ -342,12 +354,12 @@
 def join_stage(whole, pieces):
     return pl.pallas_call(
         join_kernel,
-        in_specs=[pl.BlockSpec(memory_space=pl.ANY)] + [vmem()] * DEEP,
+        in_specs=[pl.BlockSpec(memory_space=pl.ANY)] + [vmem()] * len(pieces),
         out_specs=pl.BlockSpec(memory_space=pl.ANY),
         out_shape=jax.ShapeDtypeStruct(whole.shape, F32),
-        scratch_shapes=[pltpu.SemaphoreType.DMA((DEEP,))],
+        scratch_shapes=[pltpu.SemaphoreType.DMA((len(pieces),))],
         input_output_aliases={0: 0},
-        cost_estimate=cost(1, 8 * pieces[0].size * DEEP),
+        cost_estimate=cost(1, 8 * pieces[0].size * len(pieces)),
         compiler_params=LIMIT,
         name="join_stage",
     )(whole, *pieces)
@@ -386,10 +398,14 @@
     part = zb_stage(tz[0], b[0], b[3])
     part = zb_stage(tz[1], b[1], b[2], part)
     b = north_exchange(part)
-    a = deep_exchange(ya_stage(ty, a))
-    whole = za_stage(symbol_x, tz, sy, sz, a)
-    b = deep_exchange(yb_stage(symbol_x, ty, sy, sz, b))
-    whole = join_stage(whole, b)
+    a = [deep_exchange(ya_stage(ty, a, 2 * h, 2)) for h in range(2)]
+    whole = za_stage(symbol_x, tz, sy, sz, a[0], 0)
+    parts = []
+    for part in range(2):
+        piece = yb_stage(symbol_x, ty, sy, sz, b, part, 2)
+        parts += deep_exchange(piece)
+    whole = za_stage(symbol_x, tz, sy, sz, a[1], 2, whole)
+    whole = join_stage(whole, parts)
     return whole.reshape(-1, *whole.shape[2:])
 
 

time: 135 us -> 158 us (1.17)
  waiting for transfers between devices: 52.8 us -> 67.5 us
  starting transfers between devices: 29.9 us -> 33.1 us
  Pallas kernels: 33.1 us -> 35.6 us
    ppermute x9 -> x15, waiting for transfers between devices: 32.7 us -> 43.4 us  [deep_exchange(): got[k] = lax.ppermute(pieces[k], 'deep', [(s, s ^ k) for s in range(DEEP)])]
    all_to_all x2, waiting for transfers between devices: 20 us -> 24.1 us  [north_exchange(): return lax.all_to_all(v, 'north', split_axis=0, concat_axis=0, tiled=True)]
    ppermute x9 -> x15, starting transfers between devices: 11.9 us -> 15.1 us  [deep_exchange(): got[k] = lax.ppermute(pieces[k], 'deep', [(s, s ^ k) for s in range(DEEP)])]
    pallas_call x3 -> x6, Pallas kernels: 14 us -> 16.5 us  [the longest x2 6.61 us: za_stage(): pl.pallas_call(functools.partial(za_kernel, first), grid=(js,), in_specs=...]
  transfers between devices with their start and end apart: 11 -> 17, of which waited for: 5 -> 6; matrix products, arithmetic and copies ran while one was open for 13% -> 11% of each run, Pallas kernels for 16% -> 15%
where the time goes in v3:
time: 158 us; the launch traced here: 156 us
  waiting for transfers between devices  67.5 us (43%)
  Pallas kernels  35.6 us (23%)
  starting transfers between devices  33.1 us (21%)
  other arithmetic  17.6 us (11%)
  local copies, waits for them, and re-layouts  1.62 us (1%)
    ppermute x15, waiting for transfers between devices, deep_exchange(): got[k] = lax.ppermute(pieces[k], 'deep', [(s, s ^ k) for s in range(DEEP)])  43.4 us
    all_to_all x2, waiting for transfers between devices, north_exchange(): return lax.all_to_all(v, 'north', split_axis=0, concat_axis=0, tiled=True)  24.1 us
    all_to_all x2, starting transfers between devices, north_exchange(): return lax.all_to_all(v, 'north', split_axis=0, concat_axis=0, tiled=True)  18 us
    another operation x1, other arithmetic  17.2 us
    ppermute x15, starting transfers between devices, deep_exchange(): got[k] = lax.ppermute(pieces[k], 'deep', [(s, s ^ k) for s in range(DEEP)])  15.1 us
    pallas_call x1, Pallas kernels, x_stage(): pl.pallas_call(x_kernel, grid=(steps,), in_specs=[vmem(), vmem(), pl.Bloc...  10.9 us
    pallas_call x2, Pallas kernels, zb_stage(): pl.pallas_call(zb1_kernel if first else zb2_kernel, grid=(n // rows,), in...  7.13 us
    pallas_call x2, Pallas kernels, za_stage(): pl.pallas_call(functools.partial(za_kernel, first), grid=(js,), in_specs=...  6.61 us
  transfers between devices with their start and end apart: 17, of which 6 were waited for; matrix products, arithmetic and copies ran while one was open for 11% of the time, Pallas kernels for 15%

profile of v3, /device:TPU:1, one launch (start us, length us, event | category | flops | bytes accessed | tf_op | source)
XLA Modules:
  0.0 155.7 jit_solution(13037806877782614518)
XLA Ops:
  0.0 10.9 %x_stage.1 = (f32[128,16,512]{2,1,0:T(8,128)}, f32[32,16,512]{2,1,0:T(8,128)}, f32[32,16,512]{2,1,0:T(8,128)}, f32[32,16,512]{2,1,0:T(8,128)}, f32[32,16,512]{2,1,0:T(8,128)}) custom-call(bf16[2,128,256]{2,1,0:T(8,128)(2,1)} %constant.37.clone.even_ref, bf16[2,4,32,256]{3,2,1,0:T(8,128)(2,1)} %constant.38.clone.odd_ref, f32[512,16,512]{2,1,0:T(8,128)} %x_ref.1), custom_call_target="tpu_custom_call" | custom-call | flops 3221225472 | bytes 25165824 | tf_op jit(solution)/shard_map/x_stage/pallas_call | solution.py:127
  10.9 9.5 %all-to-all-start = ((f32[32,4,16,512]{3,2,1,0:T(8,128)}), f32[32,4,16,512]{3,2,1,0:T(8,128)}, u32[]{:S(2)}, u32[]{:S(2)}) async-start(f32[32,4,16,512]{3,2,1,0:T(8,128)} %bitcast.7), calls=%async_computation | async-start | bytes 8388608 | tf_op jit(solution)/shard_map/all_to_all | solution.py:386
  20.4 2.8 %collective-permute-start.6 = (f32[32,16,512]{2,1,0:T(8,128)}, f32[32,16,512]{2,1,0:T(8,128)S(1)}, u32[]{:S(2)}, u32[]{:S(2)}) collective-permute-start(f32[32,16,512]{2,1,0:T(8,128)} %get-tuple-element.36), channel_id=1, source_target_pairs={{0,3},{1,2},{2,1},{3,0},{4,7},{5,6},{6,5},{7,4},{8,11},{9,10},{10,... | collective-permute-start | bytes 3145736 | tf_op jit(solution)/shard_map/ppermute | solution.py:381
  23.2 0.0 collective-permute-start.7
  23.3 1.3 collective-permute-start.8
  24.5 17.2 %reduce-precision_convert_fusion = (bf16[2,1,512,512]{3,2,1,0:T(8,128)(2,1)S(1)}, bf16[2,1,512,512]{3,2,1,0:T(8,128)(2,1)S(1)}, bf16[2,1,512,512]{3,2,1,0:T(8,128)(2,1)S(1)}, bf16[2,1,512,512]{3,2,1,0:T(8,128)(2,1)S(1)}) fusion(s32[512]{0:T(512)S(1)} %get-tuple-element.53, s32[2,512]{1,0:T(2,128)S(1)} %add_add_fusion, s32[512]{0:T(512)S(1)} %get-tuple-element.54), kind=kLoop, calls=%fused_computation.3 | loop fusion | flops 14680064 | bytes 4202496 | tf_op jit(solution)/shard_map/convert
  41.8 0.2 pad_maximum_fusion.1.t1_ref.table_ref
  42.0 0.0 copy-start
  42.0 0.0 copy-start.3
  42.0 0.2 pad_maximum_fusion.t0_ref.table_ref
  42.2 4.4 %collective-permute-done.6.far_ref = f32[32,16,512]{2,1,0:T(8,128)S(1)} collective-permute-done((f32[32,16,512]{2,1,0:T(8,128)}, f32[32,16,512]{2,1,0:T(8,128)S(1)}, u32[]{:S(2)}, u32[]{:S(2)}) %collective-permute-start.6) | collective-permute-done | bytes 1048608 | tf_op jit(solution)/shard_map/ppermute | solution.py:381
  46.6 0.0 copy-done.3
  46.6 2.5 %zb_stage.2.before_ref = f32[32,4,16,256]{3,2,1,0:T(8,128)S(1)} custom-call(bf16[2,2,512,512]{3,2,1,0:T(8,128)(2,1)S(1)} %pad_maximum_fusion.t0_ref.table_ref, f32[32,16,512]{2,1,0:T(8,128)S(1)} %copy-done.3, f32[32,16,512]{2,1,0:T(8,128)S(1)} %collective-permute-done.6.far_ref), custom_call_target="tpu_custom_call" | custom-call | flops 1610612736 | bytes 6291456 | tf_op jit(solution)/shard_map/zb_stage/pallas_call | solution.py:255
  49.1 0.0 collective-permute-done.7.near_ref
  49.1 21.0 %collective-permute-done.8.far_ref = f32[32,16,512]{2,1,0:T(8,128)} collective-permute-done((f32[32,16,512]{2,1,0:T(8,128)}, f32[32,16,512]{2,1,0:T(8,128)}, u32[]{:S(2)}, u32[]{:S(2)}) %collective-permute-start.8) | collective-permute-done | bytes 1048608 | tf_op jit(solution)/shard_map/ppermute | solution.py:381
  70.1 0.0 copy-done
  70.1 4.6 %zb_stage.3 = f32[32,4,16,256]{3,2,1,0:T(8,128)} custom-call(bf16[2,2,512,512]{3,2,1,0:T(8,128)(2,1)S(1)} %pad_maximum_fusion.1.t1_ref.table_ref, f32[32,4,16,256]{3,2,1,0:T(8,128)S(1)} %zb_stage.2.before_ref, f32[32,16,512]{2,1,0:T(8,128)} %collective-permute-done.7.near_ref, f32[32,16,512]{2,1,0:T(8,128)} %collective-permute-done.8.far_ref), custom_call_target="tpu_custom_call" | custom-call | flops 1610612736 | bytes 6291456 | tf_op jit(solution)/shard_map/zb_stage/pallas_call | solution.py:255
  74.8 0.0 copy-start.2
  74.8 0.0 all-to-all-done.v_ref
  74.8 8.5 %all-to-all-start.1 = ((f32[32,4,16,256]{3,2,1,0:T(8,128)}), f32[32,4,16,256]{3,2,1,0:T(8,128)}, u32[]{:S(2)}, u32[]{:S(2)}) async-start(f32[32,4,16,256]{3,2,1,0:T(8,128)} %zb_stage.3), calls=%async_computation.1 | async-start | bytes 4194304 | tf_op jit(solution)/shard_map/all_to_all | solution.py:386
  83.3 0.0 copy-done.2
  83.3 0.0 slice-start
  83.3 0.0 copy-start.9
  83.3 0.0 copy-start.4
  83.3 3.0 %ya_stage.3 = (f32[2,64,512]{2,1,0:T(8,128)S(1)}, f32[2,64,512]{2,1,0:T(8,128)}, f32[2,64,512]{2,1,0:T(8,128)S(1)}, f32[2,64,512]{2,1,0:T(8,128)S(1)}) custom-call(bf16[4,64,1536]{2,1,0:T(8,128)(2,1)S(1)} %copy-done.2, f32[32,4,16,512]{3,2,1,0:T(8,128)} %all-to-all-done.v_ref), custom_call_target="tpu_custom_call" | custom-call | flops 805306368 | bytes 3145728 | tf_op jit(solution)/shard_map/ya_stage/pallas_call | solution.py:169
  86.4 0.0 copy-start.5
  86.4 0.7 copy-done.5
  87.1 0.7 copy-done.7
  87.8 0.0 collective-permute-start.3
  87.8 0.0 slice-done
  87.8 0.1 broadcast_in_dim.6
  87.9 24.1 %all-to-all-done.1.v_ref = f32[32,4,16,256]{3,2,1,0:T(8,128)} async-done(((f32[32,4,16,256]{3,2,1,0:T(8,128)}), f32[32,4,16,256]{3,2,1,0:T(8,128)}, u32[]{:S(2)}, u32[]{:S(2)}) %all-to-all-start.1) | async-done | bytes 2097184 | tf_op jit(solution)/shard_map/all_to_all | solution.py:386
  112.0 0.1 broadcast_in_dim.7.sy_ref
  112.1 2.2 %yb_stage.3 = (f32[64,512]{1,0:T(8,128)S(1)}, f32[64,512]{1,0:T(8,128)S(1)}, f32[64,512]{1,0:T(8,128)S(1)}, f32[64,512]{1,0:T(8,128)S(1)}) custom-call(f32[512]{0:T(512)S(1)} %copy-done.4, bf16[4,64,1536]{2,1,0:T(8,128)(2,1)S(1)} %copy-done.2, f32[4,64,128]{2,1,0:T(8,128)S(1)} %broadcast_in_dim.7.sy_ref, f32[1,1024]{1,0:T(1,128)S(1)} %bitcast.3, ...), custom_call_target="tpu_custom_call" | custom-call | flops 402653184 | bytes 1572864 | tf_op jit(solution)/shard_map/yb_stage/pallas_call | solution.py:321
  114.4 0.1 collective-permute-start.12
  114.5 3.7 %collective-permute-start.4 = (f32[2,64,512]{2,1,0:T(8,128)S(1)}, f32[2,64,512]{2,1,0:T(8,128)S(1)}, u32[]{:S(2)}, u32[]{:S(2)}) collective-permute-start(f32[2,64,512]{2,1,0:T(8,128)S(1)} %copy-done.8), channel_id=1, source_target_pairs={{0,2},{1,3},{2,0},{3,1},{4,6},{5,7},{6,4},{7,5},{8,10},{9,11},{10,... | collective-permute-start | bytes 786440 | tf_op jit(solution)/shard_map/ppermute | solution.py:381
  118.2 0.0 copy-done.6
  118.2 0.1 collective-permute-start.5
  118.3 2.4 %ya_stage.2 = (f32[2,64,512]{2,1,0:T(8,128)S(1)}, f32[2,64,512]{2,1,0:T(8,128)S(1)}, f32[2,64,512]{2,1,0:T(8,128)S(1)}, f32[2,64,512]{2,1,0:T(8,128)S(1)}) custom-call(bf16[4,64,1536]{2,1,0:T(8,128)(2,1)S(1)} %copy-done.2, f32[32,4,16,512]{3,2,1,0:T(8,128)} %all-to-all-done.v_ref), custom_call_target="tpu_custom_call" | custom-call | flops 805306368 | bytes 3145728 | tf_op jit(solution)/shard_map/ya_stage/pallas_call | solution.py:169
  120.7 0.0 copy-start.1
  120.7 0.1 collective-permute-start
  120.8 0.0 collective-permute-done.12.refs_5_
  120.8 3.7 %collective-permute-start.1 = (f32[2,64,512]{2,1,0:T(8,128)S(1)}, f32[2,64,512]{2,1,0:T(8,128)S(1)}, u32[]{:S(2)}, u32[]{:S(2)}) collective-permute-start(f32[2,64,512]{2,1,0:T(8,128)S(1)} %get-tuple-element.29), channel_id=1, source_target_pairs={{0,2},{1,3},{2,0},{3,1},{4,6},{5,7},{6,4},{7,5},{8,10},{9,11},{10,... | collective-permute-start | bytes 786440 | tf_op jit(solution)/shard_map/ppermute | solution.py:381
  124.6 0.0 collective-permute-done.3.p1
  124.6 0.1 collective-permute-start.2
  124.7 2.2 %yb_stage.2 = (f32[64,512]{1,0:T(8,128)S(1)}, f32[64,512]{1,0:T(8,128)S(1)}, f32[64,512]{1,0:T(8,128)S(1)}, f32[64,512]{1,0:T(8,128)S(1)}) custom-call(f32[512]{0:T(512)S(1)} %copy-done.4, bf16[4,64,1536]{2,1,0:T(8,128)(2,1)S(1)} %copy-done.2, f32[4,64,128]{2,1,0:T(8,128)S(1)} %broadcast_in_dim.7.sy_ref, f32[1,1024]{1,0:T(1,128)S(1)} %bitcast.4, ...), custom_call_target="tpu_custom_call" | custom-call | flops 402653184 | bytes 1572864 | tf_op jit(solution)/shard_map/yb_stage/pallas_call | solution.py:321
  126.9 0.0 collective-permute-done.4.p2
  126.9 1.3 collective-permute-start.13
  128.1 3.0 %collective-permute-done.5.p3 = f32[2,64,512]{2,1,0:T(8,128)S(1)} collective-permute-done((f32[2,64,512]{2,1,0:T(8,128)S(1)}, f32[2,64,512]{2,1,0:T(8,128)S(1)}, u32[]{:S(2)}, u32[]{:S(2)}) %collective-permute-start.5) | collective-permute-done | bytes 262176 | tf_op jit(solution)/shard_map/ppermute | solution.py:381
  131.2 0.5 collective-permute-start.14
  131.7 0.0 collective-permute-done.p1
  131.7 0.5 collective-permute-start.10
  132.2 4.9 %collective-permute-done.1.p2 = f32[2,64,512]{2,1,0:T(8,128)S(1)} collective-permute-done((f32[2,64,512]{2,1,0:T(8,128)S(1)}, f32[2,64,512]{2,1,0:T(8,128)S(1)}, u32[]{:S(2)}, u32[]{:S(2)}) %collective-permute-start.1) | collective-permute-done | bytes 262176 | tf_op jit(solution)/shard_map/ppermute | solution.py:381
  137.1 0.9 collective-permute-start.11
  138.0 10.0 %collective-permute-done.2.p3 = f32[2,64,512]{2,1,0:T(8,128)S(1)} collective-permute-done((f32[2,64,512]{2,1,0:T(8,128)S(1)}, f32[2,64,512]{2,1,0:T(8,128)S(1)}, u32[]{:S(2)}, u32[]{:S(2)}) %collective-permute-start.2) | collective-permute-done | bytes 262176 | tf_op jit(solution)/shard_map/ppermute | solution.py:381
  148.0 0.0 collective-permute-start.9
  148.0 3.3 %za_stage.2.rest_0_ = f32[4,2,64,1024]{3,2,1,0:T(8,128)} custom-call(f32[512]{0:T(512)S(1)} %copy-done.4, bf16[2,2,512,512]{3,2,1,0:T(8,128)(2,1)S(1)} %pad_maximum_fusion.t0_ref.table_ref, bf16[2,2,512,512]{3,2,1,0:T(8,128)(2,1)S(1)} %copy-done.1, f32[4,64,128]{2,1,0:T(8,128)S(1)} %broadcast_in_dim.7.sy_ref, f32[1,1024]{1,0:T(1,128)S(1)} %bitcast.5, ...), custom_call_target="tpu_custom_call" | custom-call | flops 805306368 | bytes 5242880 | tf_op jit(solution)/shard_map/za_stage/pallas_call | solution.py:285
  151.4 3.3 %za_stage.3.whole_ref = f32[4,2,64,1024]{3,2,1,0:T(8,128)} custom-call(f32[512]{0:T(512)S(1)} %copy-done.4, bf16[2,2,512,512]{3,2,1,0:T(8,128)(2,1)S(1)} %pad_maximum_fusion.t0_ref.table_ref, bf16[2,2,512,512]{3,2,1,0:T(8,128)(2,1)S(1)} %copy-done.1, f32[4,64,128]{2,1,0:T(8,128)S(1)} %broadcast_in_dim.7.sy_ref, ...), custom_call_target="tpu_custom_call", output_to_operand_aliasing={{}: (9, {})} | custom-call | flops 805306368 | bytes 5242880 | tf_op jit(solution)/shard_map/za_stage/pallas_call | solution.py:285
  154.7 0.0 collective-permute-done.13.refs_6_
  154.7 0.0 collective-permute-done.14.refs_7_
  154.7 0.0 collective-permute-done.10.refs_2_
  154.7 0.0 collective-permute-done.11.refs_3_
  154.7 0.0 collective-permute-done.9.refs_1_
  154.7 1.0 join_stage.1
  (11 shorter events, 0.0 us)
Async XLA Ops:
  10.9 63.8 %all-to-all-start = ((f32[32,4,16,512]{3,2,1,0:T(8,128)}), f32[32,4,16,512]{3,2,1,0:T(8,128)}, u32[]{:S(2)}, u32[]{:S(2)}) async-start(f32[32,4,16,512]{3,2,1,0:T(8,128)} %bitcast.7), calls=%async_computation | async-start | bytes 8388608 | tf_op jit(solution)/shard_map/all_to_all | solution.py:386
  20.4 26.1 %collective-permute-start.6 = (f32[32,16,512]{2,1,0:T(8,128)}, f32[32,16,512]{2,1,0:T(8,128)S(1)}, u32[]{:S(2)}, u32[]{:S(2)}) collective-permute-start(f32[32,16,512]{2,1,0:T(8,128)} %get-tuple-element.36), channel_id=1, source_target_pairs={{0,3},{1,2},{2,1},{3,0},{4,7},{5,6},{6,5},{7,4},{8,11},{9,10},{10,... | collective-permute-start | bytes 3145736 | tf_op jit(solution)/shard_map/ppermute | solution.py:381
  23.2 25.8 %collective-permute-start.7 = (f32[32,16,512]{2,1,0:T(8,128)}, f32[32,16,512]{2,1,0:T(8,128)}, u32[]{:S(2)}, u32[]{:S(2)}) collective-permute-start(f32[32,16,512]{2,1,0:T(8,128)} %get-tuple-element.37), channel_id=1, source_target_pairs={{0,1},{1,0},{2,3},{3,2},{4,5},{5,4},{6,7},{7,6},{8,9},{9,8},{10,11... | collective-permute-start | bytes 3145736 | tf_op jit(solution)/shard_map/ppermute | solution.py:381
  23.3 46.9 %collective-permute-start.8 = (f32[32,16,512]{2,1,0:T(8,128)}, f32[32,16,512]{2,1,0:T(8,128)}, u32[]{:S(2)}, u32[]{:S(2)}) collective-permute-start(f32[32,16,512]{2,1,0:T(8,128)} %get-tuple-element.38), channel_id=1, source_target_pairs={{0,2},{1,3},{2,0},{3,1},{4,6},{5,7},{6,4},{7,5},{8,10},{9,11},{10,... | collective-permute-start | bytes 3145736 | tf_op jit(solution)/shard_map/ppermute | solution.py:381
  42.0 28.1 %copy-start = (bf16[2,2,512,512]{3,2,1,0:T(8,128)(2,1)}, bf16[2,2,512,512]{3,2,1,0:T(8,128)(2,1)S(1)}, u32[]{:S(2)}) copy-start(bf16[2,2,512,512]{3,2,1,0:T(8,128)(2,1)S(1)} %pad_maximum_fusion.1.t1_ref.table_ref) | copy-start | bytes 6291460
  42.0 4.6 %copy-start.3 = (f32[32,16,512]{2,1,0:T(8,128)S(1)}, f32[32,16,512]{2,1,0:T(8,128)}, u32[]{:S(2)}) copy-start(f32[32,16,512]{2,1,0:T(8,128)} %get-tuple-element.35.near_ref) | copy-start | bytes 3145732
  74.8 8.5 %copy-start.2 = (bf16[4,64,1536]{2,1,0:T(8,128)(2,1)S(1)}, bf16[4,64,1536]{2,1,0:T(8,128)(2,1)}, u32[]{:S(2)}) copy-start(bf16[4,64,1536]{2,1,0:T(8,128)(2,1)} %constant.39.clone.table_ref) | copy-start | bytes 2359300
  74.8 37.2 %all-to-all-start.1 = ((f32[32,4,16,256]{3,2,1,0:T(8,128)}), f32[32,4,16,256]{3,2,1,0:T(8,128)}, u32[]{:S(2)}, u32[]{:S(2)}) async-start(f32[32,4,16,256]{3,2,1,0:T(8,128)} %zb_stage.3), calls=%async_computation.1 | async-start | bytes 4194304 | tf_op jit(solution)/shard_map/all_to_all | solution.py:386
  83.3 4.5 %slice-start = ((f32[512]{0:T(512)}), f32[256]{0:T(256)S(1)}, s32[]{:S(2)}) async-start(f32[512]{0:T(512)} %param.9), calls=%async_computation.2 | async-start | bytes 2048 | tf_op jit(solution)/shard_map/slice | solution.py:396
  83.3 4.6 %copy-start.9 = (f32[2048]{0:T(1024)S(1)}, f32[2048]{0:T(1024)}, u32[]{:S(2)}) copy-start(f32[2048]{0:T(1024)} %param.10) | copy-start | bytes 24580
  83.3 28.8 %copy-start.4 = (f32[512]{0:T(512)S(1)}, f32[512]{0:T(512)}, u32[]{:S(2)}) copy-start(f32[512]{0:T(512)} %sx_ref.7) | copy-start | bytes 6148
  86.4 0.7 copy-start.5
  87.1 0.7 copy-start.7
  87.8 36.8 %collective-permute-start.3 = (f32[2,64,512]{2,1,0:T(8,128)}, f32[2,64,512]{2,1,0:T(8,128)S(1)}, u32[]{:S(2)}, u32[]{:S(2)}) collective-permute-start(f32[2,64,512]{2,1,0:T(8,128)} %get-tuple-element.32), channel_id=1, source_target_pairs={{0,1},{1,0},{2,3},{3,2},{4,5},{5,4},{6,7},{7,6},{8,9},{9,8},{10,11... | collective-permute-start | bytes 786440 | tf_op jit(solution)/shard_map/ppermute | solution.py:381
  112.0 2.4 %copy-start.8 = (f32[2,64,512]{2,1,0:T(8,128)S(1)}, f32[2,64,512]{2,1,0:T(8,128)}, u32[]{:S(2)}) copy-start(f32[2,64,512]{2,1,0:T(8,128)} %copy-done.7) | copy-start | bytes 786436
  112.0 6.2 %copy-start.6 = (f32[2,64,512]{2,1,0:T(8,128)S(1)}, f32[2,64,512]{2,1,0:T(8,128)}, u32[]{:S(2)}) copy-start(f32[2,64,512]{2,1,0:T(8,128)} %copy-done.5) | copy-start | bytes 786436
  114.4 6.5 %collective-permute-start.12 = (f32[64,512]{1,0:T(8,128)S(1)}, f32[64,512]{1,0:T(8,128)S(1)}, u32[]{:S(2)}, u32[]{:S(2)}) collective-permute-start(f32[64,512]{1,0:T(8,128)S(1)} %get-tuple-element.44), channel_id=1, source_target_pairs={{0,1},{1,0},{2,3},{3,2},{4,5},{5,4},{6,7},{7,6},{8,9},{9,8},{10,11... | collective-permute-start | bytes 393224 | tf_op jit(solution)/shard_map/ppermute | solution.py:381
  114.5 12.4 %collective-permute-start.4 = (f32[2,64,512]{2,1,0:T(8,128)S(1)}, f32[2,64,512]{2,1,0:T(8,128)S(1)}, u32[]{:S(2)}, u32[]{:S(2)}) collective-permute-start(f32[2,64,512]{2,1,0:T(8,128)S(1)} %copy-done.8), channel_id=1, source_target_pairs={{0,2},{1,3},{2,0},{3,1},{4,6},{5,7},{6,4},{7,5},{8,10},{9,11},{10,... | collective-permute-start | bytes 786440 | tf_op jit(solution)/shard_map/ppermute | solution.py:381
  118.2 13.0 %collective-permute-start.5 = (f32[2,64,512]{2,1,0:T(8,128)S(1)}, f32[2,64,512]{2,1,0:T(8,128)S(1)}, u32[]{:S(2)}, u32[]{:S(2)}) collective-permute-start(f32[2,64,512]{2,1,0:T(8,128)S(1)} %copy-done.6), channel_id=1, source_target_pairs={{0,3},{1,2},{2,1},{3,0},{4,7},{5,6},{6,5},{7,4},{8,11},{9,10},{10,... | collective-permute-start | bytes 786440 | tf_op jit(solution)/shard_map/ppermute | solution.py:381
  120.7 27.3 %copy-start.1 = (bf16[2,2,512,512]{3,2,1,0:T(8,128)(2,1)S(1)}, bf16[2,2,512,512]{3,2,1,0:T(8,128)(2,1)}, u32[]{:S(2)}) copy-start(bf16[2,2,512,512]{3,2,1,0:T(8,128)(2,1)} %copy-done) | copy-start | bytes 6291460
  120.7 10.9 %collective-permute-start = (f32[2,64,512]{2,1,0:T(8,128)S(1)}, f32[2,64,512]{2,1,0:T(8,128)S(1)}, u32[]{:S(2)}, u32[]{:S(2)}) collective-permute-start(f32[2,64,512]{2,1,0:T(8,128)S(1)} %get-tuple-element.28), channel_id=1, source_target_pairs={{0,1},{1,0},{2,3},{3,2},{4,5},{5,4},{6,7},{7,6},{8,9},{9,8},{10,11... | collective-permute-start | bytes 786440 | tf_op jit(solution)/shard_map/ppermute | solution.py:381
  120.8 16.3 %collective-permute-start.1 = (f32[2,64,512]{2,1,0:T(8,128)S(1)}, f32[2,64,512]{2,1,0:T(8,128)S(1)}, u32[]{:S(2)}, u32[]{:S(2)}) collective-permute-start(f32[2,64,512]{2,1,0:T(8,128)S(1)} %get-tuple-element.29), channel_id=1, source_target_pairs={{0,2},{1,3},{2,0},{3,1},{4,6},{5,7},{6,4},{7,5},{8,10},{9,11},{10,... | collective-permute-start | bytes 786440 | tf_op jit(solution)/shard_map/ppermute | solution.py:381
  124.6 23.4 %collective-permute-start.2 = (f32[2,64,512]{2,1,0:T(8,128)S(1)}, f32[2,64,512]{2,1,0:T(8,128)S(1)}, u32[]{:S(2)}, u32[]{:S(2)}) collective-permute-start(f32[2,64,512]{2,1,0:T(8,128)S(1)} %get-tuple-element.30), channel_id=1, source_target_pairs={{0,3},{1,2},{2,1},{3,0},{4,7},{5,6},{6,5},{7,4},{8,11},{9,10},{10,... | collective-permute-start | bytes 786440 | tf_op jit(solution)/shard_map/ppermute | solution.py:381
  126.9 27.8 %collective-permute-start.13 = (f32[64,512]{1,0:T(8,128)S(1)}, f32[64,512]{1,0:T(8,128)S(1)}, u32[]{:S(2)}, u32[]{:S(2)}) collective-permute-start(f32[64,512]{1,0:T(8,128)S(1)} %get-tuple-element.45), channel_id=1, source_target_pairs={{0,2},{1,3},{2,0},{3,1},{4,6},{5,7},{6,4},{7,5},{8,10},{9,11},{10,... | collective-permute-start | bytes 393224 | tf_op jit(solution)/shard_map/ppermute | solution.py:381
  131.2 23.5 %collective-permute-start.14 = (f32[64,512]{1,0:T(8,128)S(1)}, f32[64,512]{1,0:T(8,128)S(1)}, u32[]{:S(2)}, u32[]{:S(2)}) collective-permute-start(f32[64,512]{1,0:T(8,128)S(1)} %get-tuple-element.46), channel_id=1, source_target_pairs={{0,3},{1,2},{2,1},{3,0},{4,7},{5,6},{6,5},{7,4},{8,11},{9,10},{10,... | collective-permute-start | bytes 393224 | tf_op jit(solution)/shard_map/ppermute | solution.py:381
  131.7 23.0 %collective-permute-start.10 = (f32[64,512]{1,0:T(8,128)S(1)}, f32[64,512]{1,0:T(8,128)S(1)}, u32[]{:S(2)}, u32[]{:S(2)}) collective-permute-start(f32[64,512]{1,0:T(8,128)S(1)} %get-tuple-element.41), channel_id=1, source_target_pairs={{0,2},{1,3},{2,0},{3,1},{4,6},{5,7},{6,4},{7,5},{8,10},{9,11},{10,... | collective-permute-start | bytes 393224 | tf_op jit(solution)/shard_map/ppermute | solution.py:381
  137.1 17.6 %collective-permute-start.11 = (f32[64,512]{1,0:T(8,128)S(1)}, f32[64,512]{1,0:T(8,128)S(1)}, u32[]{:S(2)}, u32[]{:S(2)}) collective-permute-start(f32[64,512]{1,0:T(8,128)S(1)} %get-tuple-element.42), channel_id=1, source_target_pairs={{0,3},{1,2},{2,1},{3,0},{4,7},{5,6},{6,5},{7,4},{8,11},{9,10},{10,... | collective-permute-start | bytes 393224 | tf_op jit(solution)/shard_map/ppermute | solution.py:381
  148.0 6.6 %collective-permute-start.9 = (f32[64,512]{1,0:T(8,128)S(1)}, f32[64,512]{1,0:T(8,128)S(1)}, u32[]{:S(2)}, u32[]{:S(2)}) collective-permute-start(f32[64,512]{1,0:T(8,128)S(1)} %get-tuple-element.40), channel_id=1, source_target_pairs={{0,1},{1,0},{2,3},{3,2},{4,5},{5,4},{6,7},{7,6},{8,9},{9,8},{10,11... | collective-permute-start | bytes 393224 | tf_op jit(solution)/shard_map/ppermute | solution.py:381
